TPU v7x, 128 devices: a whole 4x4x4 slice. The times are simulated.
128 devices in a mesh: rows: 16 (over z_lo, y, core), width: 8 (over z_hi, x).
Axes of the slice: x: 4, y: 4, z: 4 (z_hi: 2, z_lo: 2; z = z_hi * 2 + z_lo), core: 2. Of those that a mesh axis runs over, the one named last changes fastest.
Arguments:
- one_query: float32 [7168, 7168], P('rows', 'width'), may hold values from -0.09375 to 0.09375
- other_query: float32 [7168, 7168], P('rows', 'width'), may hold values from -0.0625 to 0.0625
- one_key: float32 [7168, 1024], P('rows', 'width'), may hold values from -0.09375 to 0.09375
- other_key: float32 [7168, 1024], P('rows', 'width'), may hold values from -0.0625 to 0.0625
- one_value: float32 [7168, 1024], P('rows', 'width'), may hold values from -0.09375 to 0.09375
- other_value: float32 [7168, 1024], P('rows', 'width'), may hold values from -0.0625 to 0.0625
- mix_share: float32 [7168], P('rows'), may hold values from 0.2 to 0.8
- norm_train: float32 [7168], P(('rows', 'width')), may hold values from 0.25 to 1.75
- norm_step: float32 [7168], P(('rows', 'width')), may hold values from -0.3 to 0.3
Outputs:
- final_query: bfloat16 [7168, 7168], P(None, 'width')
- final_key: bfloat16 [7168, 1024], P(None, 'width')
- final_value: bfloat16 [7168, 1024], P(None, 'width')
- column_query: float32 [7168], P('width')
- column_key: float32 [1024], P('width')
- column_value: float32 [1024], P('width')
- serve_norm: bfloat16 [7168], replicated
All inputs are finite; a program needn't handle non-finite values.
Results may differ from a plain program's by a relative error of at most 0.001.
Values may be sent and summed in bfloat16 or wider, within the bound.
A program may use at most 128 MiB of HBM per device.

v0:
```python
import jax
import jax.numpy as jnp
from jax import lax
from jax.sharding import PartitionSpec as P


def from_everyone(x, axis):
    copies = jnp.broadcast_to(x, (lax.axis_size(axis), *x.shape))
    return lax.all_to_all(copies, axis, split_axis=0, concat_axis=0, tiled=True)


def of_everyone(x, axis):
    everything = from_everyone(x, axis)
    return jnp.sum(everything, axis=0)


def packed_total(arrays, axis):
    flat, at, finished = (jnp.concatenate([a.reshape(-1) for a in arrays]), 0, [])
    subtotal = of_everyone(flat, axis)
    for a in arrays:
        finished.append(subtotal[at : at + a.size].reshape(a.shape))
        at += a.size
    return tuple(finished)


def side_by_side(arrays, axis, dim, along):
    both = jnp.concatenate(arrays, axis=along)
    result, at, finished = (lax.all_gather(both, axis, axis=dim, tiled=True), 0, [])
    for a in arrays:
        finished.append(lax.slice_in_dim(result, at, at + a.shape[along], axis=along))
        at += a.shape[along]
    return tuple(finished)


def shards(
    one_query,
    other_query,
    one_key,
    other_key,
    one_value,
    other_value,
    mix_share,
    norm_train,
    norm_step,
):
    result_query = mix_share[:, None] * one_query + (1.0 - mix_share[:, None]) * other_query
    result_key = mix_share[:, None] * one_key + (1.0 - mix_share[:, None]) * other_key
    result_value = mix_share[:, None] * one_value + (1.0 - mix_share[:, None]) * other_value
    total_query, total_key, total_value = packed_total(
        (
            jnp.sum(result_query * result_query, axis=0),
            jnp.sum(result_key * result_key, axis=0),
            jnp.sum(result_value * result_value, axis=0),
        ),
        "rows",
    )
    column_query = jnp.sqrt(total_query)
    column_key = jnp.sqrt(total_key)
    column_value = jnp.sqrt(total_value)
    narrow_query, narrow_key, narrow_value = (
        (result_query / column_query).astype(jnp.bfloat16),
        (result_key / column_key).astype(jnp.bfloat16),
        (result_value / column_value).astype(jnp.bfloat16),
    )
    final_query, final_key, final_value = side_by_side(
        (narrow_query, narrow_key, narrow_value), "rows", 0, 1
    )
    serve_norm = lax.all_gather(
        (norm_train + norm_step).astype(jnp.bfloat16), ("rows", "width"), axis=0, tiled=True
    )
    return (final_query, final_key, final_value, column_query, column_key, column_value, serve_norm)


def solution(mesh):
    in_specs = (
        P("rows", "width"),
        P("rows", "width"),
        P("rows", "width"),
        P("rows", "width"),
        P("rows", "width"),
        P("rows", "width"),
        P("rows"),
        P(("rows", "width")),
        P(("rows", "width")),
    )
    out_specs = (
        P(None, "width"),
        P(None, "width"),
        P(None, "width"),
        P("width"),
        P("width"),
        P("width"),
        P(),
    )
    return jax.shard_map(shards, mesh=mesh, in_specs=in_specs, out_specs=out_specs, check_vma=False)
```

profile of v0, /device:TPU:1, one launch (start us, length us, event | category | flops | bytes accessed | tf_op | source)
XLA Modules:
  0.0 141.1 jit_solution(13820598020973978028)
XLA Ops:
  7.2 0.0 all-gather.2.cloned.1.call-start
  7.2 0.7 broadcast_subtract_fusion
  7.9 2.4 %multiply_reduce_fusion = f32[896]{0:T(1024)S(1)} fusion(f32[448,896]{1,0:T(8,128)} %param.10, f32[448]{0:T(512)S(1)} %broadcast_subtract_fusion, f32[448,896]{1,0:T(8,128)} %param.9, f32[448]{0:T(512)} %param.15), kind=kLoop, calls=%fused_computation.1 | loop fusion | flops 2006144 | bytes 3218432 | tf_op jit(solution)/shard_map/reduce_sum | solution.py:51
  10.3 1.5 %multiply_reduce_fusion.2 = (f32[128]{0:T(128)S(1)}, f32[128]{0:T(128)S(1)}) fusion(f32[448,128]{1,0:T(8,128)} %param.12, f32[448]{0:T(512)S(1)} %broadcast_subtract_fusion, f32[448,128]{1,0:T(8,128)} %param.11, f32[448]{0:T(512)S(1)} %copy-done.6, f32[448,128]{1,0:T(8,128)} %param.14, f32[448,128]{1,0:T(8,128)} %param.13), kind=kLoop, calls=%fused_computation.8 | loop fusion | flops 573184 | bytes 922112 | tf_op jit(solution)/shard_map/reduce_sum | solution.py:52
  11.9 13.0 %all_to_all.6 = f32[16,1,1152]{2,1,0:T(1,128)S(1)} all-to-all(f32[16,1,1152]{2,1,0:T(1,128)S(1)} %broadcast_in_dim.2), channel_id=1, replica_groups=mesh['rows'=16,'width'=8] {'rows'}, dimensions={0} | all-to-all | bytes 147456 | tf_op jit(solution)/shard_map/all_to_all | solution.py:9
  24.8 0.1 reduce_sum.39
  24.9 0.0 copy-start.8
  24.9 0.0 copy-start.9
  24.9 0.0 copy-start.7
  25.0 0.0 copy-start.3
  25.0 0.3 divide_convert_fusion
  25.3 0.2 copy-done.7
  25.5 0.4 copy-done.2
  25.9 0.1 copy-done.3
  26.0 0.1 copy-done.4
  26.1 0.1 copy-done.5
  26.2 0.2 divide_convert_fusion.2
  26.5 1.1 pad_maximum_fusion
  27.5 0.0 all-gather.2.cloned.1.call-update
  27.6 0.2 dynamic-update-slice
  27.8 65.5 %all-reduce = bf16[7168]{0:T(1024)(128)(2,1)} all-reduce(bf16[7168]{0:T(1024)(128)(2,1)S(1)} %dynamic-update-slice), channel_id=1, replica_groups=mesh['rows'=16,'width'=8] {'rows','width'}, use_global_device_ids=true, to_apply=%add | all-reduce | flops 7168 | bytes 28672
  93.3 26.1 %all-gather.2.cloned.1.call-done = bf16[7168,1152]{1,0:T(8,128)(2,1)} async-done(((bf16[448,1152]{1,0:T(8,128)(2,1)}), bf16[7168,1152]{1,0:T(8,128)(2,1)}) %all-gather.2.cloned.1.call-update) | async-done | bytes 16515088 | tf_op jit(solution)/shard_map/all_gather | solution.py:28
  119.4 10.7 %slice.27 = bf16[7168,896]{1,0:T(8,128)(2,1)} slice(bf16[7168,1152]{1,0:T(8,128)(2,1)} %all-gather.2.cloned.1.call-done), slice={[0:7168], [0:896]} | slice | bytes 25690112 | tf_op jit(solution)/shard_map/slice | solution.py:30
  130.1 4.1 %fusion = (bf16[7168,128]{1,0:T(8,128)(2,1)}, bf16[7168,128]{1,0:T(8,128)(2,1)}) fusion(bf16[7168,1152]{1,0:T(8,128)(2,1)} %all-gather.2.cloned.1.call-done), kind=kLoop, calls=%fused_computation.16 | loop fusion | bytes 7340032 | tf_op jit(solution)/shard_map/slice | solution.py:30
  (21 shorter events, 0.1 us)
Async XLA Ops:
  7.2 112.3 %all-gather.2.cloned.1.call-start = ((), (), s32[]{:S(2)}) async-start(), calls=%async_computation.1 | async-start | bytes 17547264 | tf_op jit(solution)/shard_map/all_gather | solution.py:28
  7.9 2.4 %copy-start.6 = (f32[448]{0:T(512)S(1)}, f32[448]{0:T(512)}, u32[]{:S(2)}) copy-start(f32[448]{0:T(512)} %param.15) | copy-start | bytes 5380
  7.9 17.0 %copy-start = (f32[448,896]{1,0:T(8,128)S(1)}, f32[448,896]{1,0:T(8,128)}, u32[]{:S(2)}) copy-start(f32[448,896]{1,0:T(8,128)} %param.10) | copy-start | bytes 4816900
  7.9 17.0 %copy-start.1 = (f32[448,896]{1,0:T(8,128)S(1)}, f32[448,896]{1,0:T(8,128)}, u32[]{:S(2)}) copy-start(f32[448,896]{1,0:T(8,128)} %param.9) | copy-start | bytes 4816900
  24.9 0.7 copy-start.8
  24.9 0.6 copy-start.9
  24.9 0.6 copy-start.7
  25.0 0.9 copy-start.2
  25.0 1.0 copy-start.3
  25.0 1.1 copy-start.4
  25.0 1.3 copy-start.5
  26.4 1.1 copy-start.10
  26.4 1.1 copy-start.11
Sparse Core Ops, SparseCore 0:
  27.7 91.7 all-gather.1
where the time goes:
time: 141 us
  blocking collectives  78.5 us (56%)
  waiting for transfers between devices  26.1 us (19%)
  local copies, waits for them, and re-layouts  16.1 us (11%)
  between operations  14.2 us (10%)
  other arithmetic  6.18 us (4%)
    unnamed x1, blocking collectives  65.5 us
    all_gather x1, waiting for transfers between devices, side_by_side(): lax.all_gather(both, axis, axis=dim, tiled=True)  26.1 us
    slice x2, local copies, waits for them, and re-layouts, side_by_side(): lax.slice_in_dim(result, at, at + a.shape[along], axis=along)  14.8 us
    all_to_all x1, blocking collectives, from_everyone(): return lax.all_to_all(copies, axis, split_axis=0, concat_axis=0, tiled=True)  13 us
  transfers between devices with their start and end apart: 1, of which 1 were waited for; matrix products, arithmetic and copies ran while one was open for 0% of the time, Pallas kernels for 0%

commit v1 on v0

v1 whole, which is shorter than its diff:
```python
import functools

import jax
import jax.numpy as jnp
from jax import lax
from jax.experimental import pallas as pl
from jax.experimental.pallas import tpu as pltpu
from jax.sharding import PartitionSpec as P

MESH = pl.DeviceIdType.MESH
HBM = pltpu.MemorySpace.HBM
VMEM = pltpu.MemorySpace.VMEM

UNITS = (5, 4, 5, 5, 4, 5)
OFFSETS = (0, 5, 9, 14, 19, 23)
UNIT = 16
BLOCK = 448
PIECE = 112

UP = (
    [(0, 0, c) for c in (0, 1, 2, 3, 4, 5)]
    + [(-1, 0, c) for c in (0, 1, 2)]
    + [(0, 1, c) for c in (3, 4)]
    + [(-1, 1, c) for c in (0, 1, 2)]
)
DOWN = (
    [(0, 0, c) for c in (3, 4, 5, 0, 1, 2)]
    + [(1, 0, c) for c in (3, 4, 5)]
    + [(0, 1, c) for c in (0, 1)]
    + [(1, 1, c) for c in (3, 4, 5)]
)
ACROSS = (
    [(0, 0, c) for c in (0, 3, 1, 4, 2, 5)]
    + [(-1, 0, 0), (1, 0, 3), (-1, 0, 1), (1, 0, 4), (-1, 0, 2), (1, 0, 5), (-1, 0, 5), (1, 0, 2)]
)
SENT = (UP, DOWN, ACROSS)
SHIFT = ((1, 0), (-1, 0), (0, 1))
STEPS = len(UP)
AHEAD = 3


def arriving(link, step):
    dy, dz, chunk = SENT[link][step]
    sy, sz = SHIFT[link]
    return ((dy - sy) % 4, (dz - sz) % 2, chunk)


ARRIVAL = {arriving(l, s): (l, s) for l in range(3) for s in range(STEPS)}
EVENTS = [(0, 0, c) for c in range(6)]


def gather_kernel(
    one_query,
    other_query,
    one_key,
    other_key,
    one_value,
    other_value,
    share,
    train,
    step_gain,
    gathered,
    scales,
    gain,
    first,
    second,
    share_row,
    share_tile,
    sums,
    inverse,
    gain_tile,
    gain_rows,
    gain_flat,
    load_sem,
    sum_send,
    sum_recv,
    across_send,
    across_recv,
    gain_send,
    gain_recv,
    link_send,
    link_recv,
    core_send,
    core_recv,
):
    me = lax.axis_index("rows")
    column = lax.axis_index("width")
    core = lax.rem(me, 2)
    y = lax.rem(me // 2, 4)
    z = me // 8

    def device(dy, dz, on):
        return lax.rem(z + dz + 2, 2) * 8 + lax.rem(y + dy + 4, 4) * 2 + on

    pieces = BLOCK // PIECE
    sources = (
        (one_query, first, 0, 896),
        (other_query, second, 0, 896),
        (one_key, first, 896, 128),
        (other_key, second, 896, 128),
        (one_value, first, 1024, 128),
        (other_value, second, 1024, 128),
    )

    def load(piece, number):
        source, target, at, width = sources[number]
        rows = pl.ds(piece * PIECE, PIECE)
        return pltpu.make_async_copy(
            source.at[rows, :], target.at[rows, pl.ds(at, width)], load_sem.at[piece, number]
        )

    for piece in range(pieces):
        for number in range(6):
            load(piece, number).start()

    barrier = pltpu.get_barrier_semaphore()
    for k in range(1, 16):
        pl.semaphore_signal(barrier, inc=1, device_id=(lax.rem(me + k, 16), column), device_id_type=MESH)
    for k in range(1, 8):
        pl.semaphore_signal(barrier, inc=1, device_id=(me, lax.rem(column + k, 8)), device_id_type=MESH)

    share_row[...] = jnp.zeros_like(share_row)
    share_row[:, 0:BLOCK] = share[...]
    for part in range(4):
        lanes = share_row[:, part * 128 : (part + 1) * 128]
        share_tile[pl.ds(part * 128, 128), :] = jnp.transpose(jnp.broadcast_to(lanes, (128, 128)))

    gain_tile[...] = jnp.zeros_like(gain_tile)
    gain_tile[0:1, 0:56] = (train[...] + step_gain[...]).astype(jnp.bfloat16).astype(jnp.float32)
    place = lax.rem(56 * (lax.rem(me, 2) * 8 + column), 128)
    gain_rows[me, column] = pltpu.roll(gain_tile[...], place, 1)[0:1, :]

    def mix(piece):
        def body(i, total):
            total = list(total)
            for half in range(2):
                rows = pl.ds(pl.multiple_of(piece * PIECE + i * 16 + half * 8, 8), 8)
                mine = share_tile[rows, :]
                rest = 1.0 - mine
                for j in range(9):
                    lanes = slice(j * 128, (j + 1) * 128)
                    result = mine * first[rows, lanes] + rest * second[rows, lanes]
                    first[rows, lanes] = result
                    total[j] = total[j] + result * result
            return tuple(total)

        return body

    total = tuple(jnp.zeros((8, 128), jnp.float32) for _ in range(9))
    for piece in range(pieces):
        for number in range(6):
            load(piece, number).wait()
        total = lax.fori_loop(0, PIECE // 16, mix(piece), total)
    for j in range(9):
        sums[me, j] = jnp.sum(total[j], axis=0, keepdims=True)

    pl.semaphore_wait(barrier, 22)

    def send_sum(k, owner):
        return pltpu.make_async_remote_copy(
            src_ref=sums.at[owner],
            dst_ref=sums.at[owner],
            send_sem=sum_send.at[k],
            recv_sem=sum_recv.at[k],
            device_id=(lax.rem(me + k, 16), column),
            device_id_type=MESH,
        )

    def send_across(k, owner):
        return pltpu.make_async_remote_copy(
            src_ref=gain_rows.at[me, owner],
            dst_ref=gain_rows.at[me, owner],
            send_sem=across_send.at[k],
            recv_sem=across_recv.at[k],
            device_id=(me, lax.rem(column + k, 8)),
            device_id_type=MESH,
        )

    def send_gain(k, owner):
        return pltpu.make_async_remote_copy(
            src_ref=gain_rows.at[owner],
            dst_ref=gain_rows.at[owner],
            send_sem=gain_send.at[k],
            recv_sem=gain_recv.at[k],
            device_id=(lax.rem(me + k, 16), column),
            device_id_type=MESH,
        )

    for k in range(1, 16):
        send_sum(k, me).start()
    for k in range(1, 8):
        send_across(k, column).start()
    for k in range(1, 16):
        send_sum(k, lax.rem(me + 16 - k, 16)).wait_recv()

    grand = [sums[0, j] for j in range(9)]
    for other in range(1, 16):
        grand = [grand[j] + sums[other, j] for j in range(9)]
    for j in range(9):
        scale = jnp.sqrt(grand[j])
        scales[j] = scale
        inverse[j] = 1.0 / scale

    def rows_of(dy, dz, chunk, on):
        start = device(dy, dz, on) * BLOCK + OFFSETS[chunk] * UNIT
        return pl.ds(pl.multiple_of(start, UNIT), UNITS[chunk] * UNIT)

    def link_copy(link, step, item):
        rows = rows_of(*item, core)
        sy, sz = SHIFT[link]
        return pltpu.make_async_remote_copy(
            src_ref=gathered.at[rows, :],
            dst_ref=gathered.at[rows, :],
            send_sem=link_send.at[link, step],
            recv_sem=link_recv.at[link, step],
            device_id=(device(sy, sz, core), column),
            device_id_type=MESH,
        )

    events = []

    def core_copy(event, item, on):
        rows = rows_of(*item, on)
        return pltpu.make_async_remote_copy(
            src_ref=gathered.at[rows, :],
            dst_ref=gathered.at[rows, :],
            send_sem=core_send.at[event],
            recv_sem=core_recv.at[event],
            device_id=(device(0, 0, 1 - core), column),
            device_id_type=MESH,
        )

    def hand_over(item):
        core_copy(len(events), item, core).start()
        events.append(item)

    def normalise(chunk):
        def body(i, _):
            at = pl.multiple_of(OFFSETS[chunk] * UNIT + i * UNIT, UNIT)
            to = pl.multiple_of(me * BLOCK + OFFSETS[chunk] * UNIT + i * UNIT, UNIT)
            for j in range(9):
                lanes = slice(j * 128, (j + 1) * 128)
                gathered[pl.ds(to, UNIT), lanes] = (first[pl.ds(at, UNIT), lanes] * inverse[j]).astype(jnp.bfloat16)
            return 0

        lax.fori_loop(0, UNITS[chunk], body, 0)

    for chunk in (0, 3, 1, 4, 2, 5):
        normalise(chunk)

    arrived = set()

    def receive(link, step):
        if (link, step) in arrived:
            return
        arrived.add((link, step))
        item = arriving(link, step)
        link_copy(link, step, item).wait_recv()
        hand_over(item)

    for step in range(STEPS):
        for link in range(3):
            if step >= AHEAD:
                link_copy(link, step - AHEAD, SENT[link][step - AHEAD]).wait_send()
            dy, dz, chunk = SENT[link][step]
            if (dy, dz) != (0, 0):
                receive(*ARRIVAL[dy % 4, dz % 2, chunk])
            link_copy(link, step, SENT[link][step]).start()
        if step < 6:
            hand_over((0, 0, step))
        if step == 2:
            for k in range(1, 8):
                send_across(k, lax.rem(column + 8 - k, 8)).wait_recv()
            for k in range(1, 16):
                send_gain(k, me).start()
        if step >= AHEAD:
            for link in range(3):
                receive(link, step - AHEAD)

    for k in range(1, 16):
        send_gain(k, lax.rem(me + 16 - k, 16)).wait_recv()
    lane = lax.broadcasted_iota(jnp.int32, (1, 128), 1)
    for group in range(8):
        rows = [jnp.zeros((1, 128), jnp.float32) for _ in range(8)]
        for j in range(16):
            values = gain_rows[group * 2 + j // 8, j % 8]
            row, at = (56 * j) // 128, (56 * j) % 128
            rows[row] = jnp.where((lane >= at) & (lane < at + 56), values, rows[row])
            if at + 56 > 128:
                rows[row + 1] = jnp.where(lane < at + 56 - 128, values, rows[row + 1])
        for row in range(7):
            gain_flat[group * 7 + row : group * 7 + row + 1, :] = rows[row]
    gain[...] = gain_flat[...].astype(jnp.bfloat16)

    for step in range(STEPS - AHEAD, STEPS):
        for link in range(3):
            receive(link, step)
    for event, item in enumerate(events):
        core_copy(event, item, 1 - core).wait_recv()
    for step in range(STEPS - AHEAD, STEPS):
        for link in range(3):
            link_copy(link, step, SENT[link][step]).wait_send()
    for event, item in enumerate(events):
        core_copy(event, item, core).wait_send()
    for k in range(1, 16):
        send_sum(k, me).wait_send()
        send_gain(k, me).wait_send()
    for k in range(1, 8):
        send_across(k, column).wait_send()


def write_kernel(gathered, query, key, value, sem):
    copies = []
    parts = 8
    rows = gathered.shape[0] // parts
    for part in range(parts):
        for target, at, width in ((query, 0, 896), (key, 896, 128), (value, 1024, 128)):
            copies.append(
                pltpu.make_async_copy(
                    gathered.at[pl.ds(part * rows, rows), pl.ds(at, width)],
                    target.at[pl.ds(part * rows, rows), :],
                    sem.at[len(copies)],
                )
            )
    for copy in copies:
        copy.start()
    for copy in copies:
        copy.wait()


def shards(
    one_query,
    other_query,
    one_key,
    other_key,
    one_value,
    other_value,
    mix_share,
    norm_train,
    norm_step,
):
    dma = pltpu.SemaphoreType.DMA
    weights = [
        pltpu.with_memory_space_constraint(w, HBM)
        for w in (one_query, other_query, one_key, other_key, one_value, other_value)
    ]
    gathered, scales, gain = pl.pallas_call(
        gather_kernel,
        out_shape=(
            jax.ShapeDtypeStruct((7168, 1152), jnp.bfloat16),
            jax.ShapeDtypeStruct((9, 1, 128), jnp.float32),
            jax.ShapeDtypeStruct((56, 128), jnp.bfloat16),
        ),
        in_specs=[pl.BlockSpec(memory_space=HBM)] * 6 + [pl.BlockSpec(memory_space=VMEM)] * 3,
        out_specs=(pl.BlockSpec(memory_space=VMEM),) * 3,
        scratch_shapes=[
            pltpu.VMEM((448, 1152), jnp.float32),
            pltpu.VMEM((448, 1152), jnp.float32),
            pltpu.VMEM((1, 512), jnp.float32),
            pltpu.VMEM((512, 128), jnp.float32),
            pltpu.VMEM((16, 9, 1, 128), jnp.float32),
            pltpu.VMEM((9, 1, 128), jnp.float32),
            pltpu.VMEM((8, 128), jnp.float32),
            pltpu.VMEM((16, 8, 1, 128), jnp.float32),
            pltpu.VMEM((56, 128), jnp.float32),
            dma((4, 6)),
            dma((16,)),
            dma((16,)),
            dma((8,)),
            dma((8,)),
            dma((16,)),
            dma((16,)),
            dma((3, STEPS)),
            dma((3, STEPS)),
            dma((48,)),
            dma((48,)),
        ],
        compiler_params=pltpu.CompilerParams(
            collective_id=0, has_side_effects=True, vmem_limit_bytes=32 << 20
        ),
    )(
        *weights,
        mix_share.reshape(1, 448),
        norm_train.reshape(1, 56),
        norm_step.reshape(1, 56),
    )
    query, key, value = pl.pallas_call(
        write_kernel,
        out_shape=(
            jax.ShapeDtypeStruct((7168, 896), jnp.bfloat16),
            jax.ShapeDtypeStruct((7168, 128), jnp.bfloat16),
            jax.ShapeDtypeStruct((7168, 128), jnp.bfloat16),
        ),
        in_specs=[pl.BlockSpec(memory_space=VMEM)],
        out_specs=(pl.BlockSpec(memory_space=HBM),) * 3,
        scratch_shapes=[dma((24,))],
        compiler_params=pltpu.CompilerParams(vmem_limit_bytes=20 << 20),
    )(gathered)
    flat = scales.reshape(1152)
    return (query, key, value, flat[:896], flat[896:1024], flat[1024:], gain.reshape(7168))


def solution(mesh):
    in_specs = (
        P("rows", "width"),
        P("rows", "width"),
        P("rows", "width"),
        P("rows", "width"),
        P("rows", "width"),
        P("rows", "width"),
        P("rows"),
        P(("rows", "width")),
        P(("rows", "width")),
    )
    out_specs = (
        P(None, "width"),
        P(None, "width"),
        P(None, "width"),
        P("width"),
        P("width"),
        P("width"),
        P(),
    )
    return jax.shard_map(shards, mesh=mesh, in_specs=in_specs, out_specs=out_specs, check_vma=False)
```

time: 141 us -> 82.7 us (0.59)
  blocking collectives: 78.5 us -> 0 us
  Pallas kernels: 0 us -> 78.1 us
  waiting for transfers between devices: 26.1 us -> 0 us
  between operations: 14.2 us -> 0.66 us
  local copies, waits for them, and re-layouts: 16.1 us -> 3.71 us
  other arithmetic: 6.18 us -> 0 us
    pallas_call x0 -> x2, Pallas kernels: none -> 78.1 us  [the longest x1 72.2 us: shards(): pl.pallas_call(gather_kernel, out_shape=(jax.ShapeDtypeStruct((7168, 1152...]
    unnamed x1 -> x0, blocking collectives: 65.5 us -> none
    all_gather x1 -> x0, waiting for transfers between devices: 26.1 us -> none  [side_by_side(): lax.all_gather(both, axis, axis=dim, tiled=True)]
    slice x2, local copies, waits for them, and re-layouts: 14.8 us -> 1.12 us  [the longest x1 0.61 us: shards(): flat[:896]]
    all_to_all x1 -> x0, blocking collectives: 13 us -> none  [from_everyone(): return lax.all_to_all(copies, axis, split_axis=0, concat_axis=0, tiled=True)]
    reduce_sum x3 -> x0, other arithmetic: 3.92 us -> none  [the longest x1 2.39 us: shards(): jnp.sum(result_query * result_query, axis=0)]
  transfers between devices with their start and end apart: 1 -> 0, of which waited for: 1 -> 0; matrix products, arithmetic and copies ran while one was open for 0% -> 0% of each run, Pallas kernels for 0% -> 0%
where the time goes in v1:
time: 82.7 us; the launch traced here: 82.5 us
  Pallas kernels  78.1 us (94%)
  local copies, waits for them, and re-layouts  3.71 us (4%)
    pallas_call x1, Pallas kernels, shards(): pl.pallas_call(gather_kernel, out_shape=(jax.ShapeDtypeStruct((7168, 1152...  72.2 us
    pallas_call x1, Pallas kernels, shards(): pl.pallas_call(write_kernel, out_shape=(jax.ShapeDtypeStruct((7168, 896),...  5.96 us
    unnamed x7, local copies, waits for them, and re-layouts  2.59 us

profile of v1, /device:TPU:1, one launch (start us, length us, event | category | flops | bytes accessed | tf_op | source)
XLA Modules:
  0.0 82.5 jit_solution(18128851015403265037)
XLA Ops:
  0.6 0.0 copy-start
  0.6 0.7 copy-done
  1.3 0.0 copy-start.1
  1.3 0.7 copy-done.1
  2.0 0.0 copy-start.2
  2.0 0.7 copy-done.2
  2.6 72.2 %shard_map.144 = (bf16[7168,1152]{1,0:T(8,128)(2,1)S(1)}, f32[9,1,128]{2,1,0:T(1,128)S(1)}, bf16[56,128]{1,0:T(8,128)(2,1)S(1)}) custom-call(f32[448,896]{1,0:T(8,128)} %one_query.1, f32[448,896]{1,0:T(8,128)} %other_query.1, f32[448,128]{1,0:T(8,128)} %one_key.1, f32[448,128]{1,0:T(8,128)} %other_key.1, f32[448,128]{1,0:T(8,128)} %one_value.1, ...), custom_call_target="tpu_custom_call" | custom-call | tf_op jit(solution)/shard_map/pallas_call | solution.py:347
  74.8 6.0 %shard_map.145 = (bf16[7168,896]{1,0:T(8,128)(2,1)}, bf16[7168,128]{1,0:T(8,128)(2,1)}, bf16[7168,128]{1,0:T(8,128)(2,1)}) custom-call(bf16[7168,1152]{1,0:T(8,128)(2,1)S(1)} %get-tuple-element.13.gathered), custom_call_target="tpu_custom_call" | custom-call | tf_op jit(solution)/shard_map/pallas_call | solution.py:387
  80.8 0.5 slice_bitcast_fusion
  81.3 0.6 slice_reduce_fusion
  81.9 0.6 copy.17
Async XLA Ops:
  0.6 0.7 copy-start
  1.3 0.7 copy-start.1
  2.0 0.7 copy-start.2

commit v2 on v1

--- a/solution.py
+++ b/solution.py
@@ -37,6 +37,9 @@
 SHIFT = ((1, 0), (-1, 0), (0, 1))
 STEPS = len(UP)
 AHEAD = 3
+GATE = 5
+GAIN_STEPS = (4, 7, 8, 11)
+FARTHEST = ((2, 1), (1, 1), (3, 1), (2, 0), (1, 0), (3, 0), (0, 1), (0, 0))
 
 
 def arriving(link, step):
@@ -56,14 +59,19 @@
     other_key,
     one_value,
     other_value,
+    share_input,
+    train_input,
+    step_input,
+    gathered,
+    scale_query,
+    scale_key,
+    scale_value,
+    gain,
+    first,
+    second,
     share,
     train,
     step_gain,
-    gathered,
-    scales,
-    gain,
-    first,
-    second,
     share_row,
     share_tile,
     sums,
@@ -72,10 +80,14 @@
     gain_rows,
     gain_flat,
     load_sem,
+    small_sem,
+    entered,
     sum_send,
     sum_recv,
-    across_send,
-    across_recv,
+    row_send,
+    row_recv,
+    gate_send,
+    gate_recv,
     gain_send,
     gain_recv,
     link_send,
@@ -109,15 +121,34 @@
             source.at[rows, :], target.at[rows, pl.ds(at, width)], load_sem.at[piece, number]
         )
 
+    small = [
+        pltpu.make_async_copy(source, target, small_sem.at[number])
+        for number, (source, target) in enumerate(
+            ((share_input, share), (train_input, train), (step_input, step_gain))
+        )
+    ]
+    for copy in small:
+        copy.start()
     for piece in range(pieces):
         for number in range(6):
             load(piece, number).start()
 
+    at_gate = me == GATE
     barrier = pltpu.get_barrier_semaphore()
     for k in range(1, 16):
-        pl.semaphore_signal(barrier, inc=1, device_id=(lax.rem(me + k, 16), column), device_id_type=MESH)
-    for k in range(1, 8):
-        pl.semaphore_signal(barrier, inc=1, device_id=(me, lax.rem(column + k, 8)), device_id_type=MESH)
+        peer = lax.rem(me + k, 16)
+
+        @pl.when(peer != GATE)
+        def _():
+            pl.semaphore_signal(barrier, inc=1, device_id=(peer, column), device_id_type=MESH)
+
+    @pl.when(at_gate)
+    def _():
+        for k in range(1, 8):
+            pl.semaphore_signal(barrier, inc=1, device_id=(me, lax.rem(column + k, 8)), device_id_type=MESH)
+
+    for copy in small:
+        copy.wait()
 
     share_row[...] = jnp.zeros_like(share_row)
     share_row[:, 0:BLOCK] = share[...]
@@ -128,7 +159,7 @@
     gain_tile[...] = jnp.zeros_like(gain_tile)
     gain_tile[0:1, 0:56] = (train[...] + step_gain[...]).astype(jnp.bfloat16).astype(jnp.float32)
     place = lax.rem(56 * (lax.rem(me, 2) * 8 + column), 128)
-    gain_rows[me, column] = pltpu.roll(gain_tile[...], place, 1)[0:1, :]
+    gain_rows[column, me] = pltpu.roll(gain_tile[...], place, 1)[0:1, :]
 
     def mix(piece):
         def body(i, total):
@@ -154,52 +185,100 @@
     for j in range(9):
         sums[me, j] = jnp.sum(total[j], axis=0, keepdims=True)
 
-    pl.semaphore_wait(barrier, 22)
+    @pl.when(jnp.logical_not(at_gate))
+    def _():
+        pl.semaphore_wait(barrier, 15)
+
+    @pl.when(me == GATE - 1)
+    def _():
+        pl.semaphore_signal(entered, inc=1, device_id=(GATE, column), device_id_type=MESH)
+
+    @pl.when(at_gate)
+    def _():
+        pl.semaphore_wait(entered, 1)
+
+    others = [(dy, dz, on) for dy, dz in FARTHEST for on in (0, 1) if (dy, dz, on) != (0, 0, 0)]
 
     def send_sum(k, owner):
+        dy, dz, on = others[k]
         return pltpu.make_async_remote_copy(
             src_ref=sums.at[owner],
             dst_ref=sums.at[owner],
             send_sem=sum_send.at[k],
             recv_sem=sum_recv.at[k],
-            device_id=(lax.rem(me + k, 16), column),
+            device_id=(device(dy, dz, lax.rem(core + on, 2)), column),
             device_id_type=MESH,
         )
 
-    def send_across(k, owner):
+    for k in range(15):
+        send_sum(k, me).start()
+
+    def send_row(owner):
         return pltpu.make_async_remote_copy(
-            src_ref=gain_rows.at[me, owner],
-            dst_ref=gain_rows.at[me, owner],
-            send_sem=across_send.at[k],
-            recv_sem=across_recv.at[k],
-            device_id=(me, lax.rem(column + k, 8)),
+            src_ref=gain_rows.at[column, owner],
+            dst_ref=gain_rows.at[column, owner],
+            send_sem=row_send,
+            recv_sem=row_recv.at[owner],
+            device_id=(GATE, column),
             device_id_type=MESH,
         )
 
-    def send_gain(k, owner):
+    def send_group(k, owner):
         return pltpu.make_async_remote_copy(
             src_ref=gain_rows.at[owner],
             dst_ref=gain_rows.at[owner],
+            send_sem=gate_send.at[k],
+            recv_sem=gate_recv.at[k],
+            device_id=(GATE, lax.rem(column + k, 8)),
+            device_id_type=MESH,
+        )
+
+    def send_gain(k, to):
+        return pltpu.make_async_remote_copy(
+            src_ref=gain,
+            dst_ref=gain,
             send_sem=gain_send.at[k],
-            recv_sem=gain_recv.at[k],
-            device_id=(lax.rem(me + k, 16), column),
+            recv_sem=gain_recv,
+            device_id=(to, column),
             device_id_type=MESH,
         )
 
-    for k in range(1, 16):
-        send_sum(k, me).start()
-    for k in range(1, 8):
-        send_across(k, column).start()
-    for k in range(1, 16):
-        send_sum(k, lax.rem(me + 16 - k, 16)).wait_recv()
+    @pl.when(jnp.logical_not(at_gate))
+    def _():
+        send_row(me).start()
+
+    for k in range(15):
+        dy, dz, on = others[k]
+        send_sum(k, device(-dy, -dz, lax.rem(core + on, 2))).wait_recv()
 
     grand = [sums[0, j] for j in range(9)]
     for other in range(1, 16):
         grand = [grand[j] + sums[other, j] for j in range(9)]
     for j in range(9):
         scale = jnp.sqrt(grand[j])
-        scales[j] = scale
+        if j < 7:
+            scale_query[j : j + 1, :] = scale
+        elif j == 7:
+            scale_key[...] = scale
+        else:
+            scale_value[...] = scale
         inverse[j] = 1.0 / scale
+
+    def compose():
+        lane = lax.broadcasted_iota(jnp.int32, (1, 128), 1)
+        for group in range(8):
+            rows = [jnp.zeros((1, 128), jnp.float32) for _ in range(8)]
+            for j in range(16):
+                values = gain_rows[j % 8, group * 2 + j // 8]
+                row, at = (56 * j) // 128, (56 * j) % 128
+                rows[row] = jnp.where((lane >= at) & (lane < at + 56), values, rows[row])
+                if at + 56 > 128:
+                    rows[row + 1] = jnp.where(lane < at + 56 - 128, values, rows[row + 1])
+            for row in range(7):
+                gain_flat[group * 7 + row : group * 7 + row + 1, :] = rows[row]
+        gain[...] = gain_flat[...].astype(jnp.bfloat16)
+
+    spread = [to for to in range(16) if to % 2 == GATE % 2 and to != GATE] + [GATE - 1]
 
     def rows_of(dy, dz, chunk, on):
         start = device(dy, dz, on) * BLOCK + OFFSETS[chunk] * UNIT
@@ -268,29 +347,42 @@
             link_copy(link, step, SENT[link][step]).start()
         if step < 6:
             hand_over((0, 0, step))
-        if step == 2:
-            for k in range(1, 8):
-                send_across(k, lax.rem(column + 8 - k, 8)).wait_recv()
-            for k in range(1, 16):
-                send_gain(k, me).start()
+        if step == GAIN_STEPS[0]:
+
+            @pl.when(at_gate)
+            def _():
+                for owner in range(16):
+                    if owner != GATE:
+                        send_row(owner).wait_recv()
+                pl.semaphore_wait(barrier, 7)
+                for k in range(1, 8):
+                    send_group(k, column).start()
+
+        if step == GAIN_STEPS[1]:
+
+            @pl.when(at_gate)
+            def _():
+                for k in range(1, 8):
+                    send_group(k, lax.rem(column + 8 - k, 8)).wait_recv()
+                compose()
+
+        if step == GAIN_STEPS[2]:
+
+            @pl.when(at_gate)
+            def _():
+                for k, to in enumerate(spread):
+                    send_gain(k, to).start()
+
+        if step == GAIN_STEPS[3]:
+
+            @pl.when(jnp.logical_and(jnp.logical_not(at_gate), core == GATE % 2))
+            def _():
+                send_gain(0, me).wait_recv()
+                send_gain(0, device(0, 0, 1 - core)).start()
+
         if step >= AHEAD:
             for link in range(3):
                 receive(link, step - AHEAD)
-
-    for k in range(1, 16):
-        send_gain(k, lax.rem(me + 16 - k, 16)).wait_recv()
-    lane = lax.broadcasted_iota(jnp.int32, (1, 128), 1)
-    for group in range(8):
-        rows = [jnp.zeros((1, 128), jnp.float32) for _ in range(8)]
-        for j in range(16):
-            values = gain_rows[group * 2 + j // 8, j % 8]
-            row, at = (56 * j) // 128, (56 * j) % 128
-            rows[row] = jnp.where((lane >= at) & (lane < at + 56), values, rows[row])
-            if at + 56 > 128:
-                rows[row + 1] = jnp.where(lane < at + 56 - 128, values, rows[row + 1])
-        for row in range(7):
-            gain_flat[group * 7 + row : group * 7 + row + 1, :] = rows[row]
-    gain[...] = gain_flat[...].astype(jnp.bfloat16)
 
     for step in range(STEPS - AHEAD, STEPS):
         for link in range(3):
@@ -302,30 +394,47 @@
             link_copy(link, step, SENT[link][step]).wait_send()
     for event, item in enumerate(events):
         core_copy(event, item, core).wait_send()
-    for k in range(1, 16):
+    for k in range(15):
         send_sum(k, me).wait_send()
-        send_gain(k, me).wait_send()
-    for k in range(1, 8):
-        send_across(k, column).wait_send()
-
-
-def write_kernel(gathered, query, key, value, sem):
+
+    @pl.when(core != GATE % 2)
+    def _():
+        send_gain(0, me).wait_recv()
+
+    @pl.when(at_gate)
+    def _():
+        for k in range(1, 8):
+            send_group(k, column).wait_send()
+        for k, to in enumerate(spread):
+            send_gain(k, to).wait_send()
+
+    @pl.when(jnp.logical_not(at_gate))
+    def _():
+        send_row(me).wait_send()
+
+        @pl.when(core == GATE % 2)
+        def _():
+            send_gain(0, me).wait_send()
+
+
+def write_kernel(gathered, *rest):
+    small, (query, key, value), outs, sem = rest[:4], rest[4:7], rest[7:11], rest[11]
     copies = []
+
+    def copy(source, target):
+        copies.append(pltpu.make_async_copy(source, target, sem.at[len(copies)]))
+
     parts = 8
     rows = gathered.shape[0] // parts
     for part in range(parts):
         for target, at, width in ((query, 0, 896), (key, 896, 128), (value, 1024, 128)):
-            copies.append(
-                pltpu.make_async_copy(
-                    gathered.at[pl.ds(part * rows, rows), pl.ds(at, width)],
-                    target.at[pl.ds(part * rows, rows), :],
-                    sem.at[len(copies)],
-                )
-            )
-    for copy in copies:
-        copy.start()
-    for copy in copies:
-        copy.wait()
+            copy(gathered.at[pl.ds(part * rows, rows), pl.ds(at, width)], target.at[pl.ds(part * rows, rows), :])
+    for source, target in zip(small, outs):
+        copy(source, target)
+    for one in copies:
+        one.start()
+    for one in copies:
+        one.wait()
 
 
 def shards(
@@ -340,36 +449,56 @@
     norm_step,
 ):
     dma = pltpu.SemaphoreType.DMA
-    weights = [
-        pltpu.with_memory_space_constraint(w, HBM)
-        for w in (one_query, other_query, one_key, other_key, one_value, other_value)
+    f32, bf16 = jnp.float32, jnp.bfloat16
+    inputs = [
+        pltpu.with_memory_space_constraint(x, HBM)
+        for x in (
+            one_query,
+            other_query,
+            one_key,
+            other_key,
+            one_value,
+            other_value,
+            mix_share.reshape(1, 448),
+            norm_train.reshape(1, 56),
+            norm_step.reshape(1, 56),
+        )
     ]
-    gathered, scales, gain = pl.pallas_call(
+    small = (
+        jax.ShapeDtypeStruct((7, 128), f32),
+        jax.ShapeDtypeStruct((1, 128), f32),
+        jax.ShapeDtypeStruct((1, 128), f32),
+        jax.ShapeDtypeStruct((56, 128), bf16),
+    )
+    gathered, *rest = pl.pallas_call(
         gather_kernel,
-        out_shape=(
-            jax.ShapeDtypeStruct((7168, 1152), jnp.bfloat16),
-            jax.ShapeDtypeStruct((9, 1, 128), jnp.float32),
-            jax.ShapeDtypeStruct((56, 128), jnp.bfloat16),
-        ),
-        in_specs=[pl.BlockSpec(memory_space=HBM)] * 6 + [pl.BlockSpec(memory_space=VMEM)] * 3,
-        out_specs=(pl.BlockSpec(memory_space=VMEM),) * 3,
+        out_shape=(jax.ShapeDtypeStruct((7168, 1152), bf16), *small),
+        in_specs=[pl.BlockSpec(memory_space=HBM)] * 9,
+        out_specs=(pl.BlockSpec(memory_space=VMEM),) * 5,
         scratch_shapes=[
-            pltpu.VMEM((448, 1152), jnp.float32),
-            pltpu.VMEM((448, 1152), jnp.float32),
-            pltpu.VMEM((1, 512), jnp.float32),
-            pltpu.VMEM((512, 128), jnp.float32),
-            pltpu.VMEM((16, 9, 1, 128), jnp.float32),
-            pltpu.VMEM((9, 1, 128), jnp.float32),
-            pltpu.VMEM((8, 128), jnp.float32),
-            pltpu.VMEM((16, 8, 1, 128), jnp.float32),
-            pltpu.VMEM((56, 128), jnp.float32),
+            pltpu.VMEM((448, 1152), f32),
+            pltpu.VMEM((448, 1152), f32),
+            pltpu.VMEM((1, 448), f32),
+            pltpu.VMEM((1, 56), f32),
+            pltpu.VMEM((1, 56), f32),
+            pltpu.VMEM((1, 512), f32),
+            pltpu.VMEM((512, 128), f32),
+            pltpu.VMEM((16, 9, 1, 128), f32),
+            pltpu.VMEM((9, 1, 128), f32),
+            pltpu.VMEM((8, 128), f32),
+            pltpu.VMEM((8, 16, 1, 128), f32),
+            pltpu.VMEM((56, 128), f32),
             dma((4, 6)),
-            dma((16,)),
+            dma((3,)),
+            pltpu.SemaphoreType.REGULAR,
+            dma((15,)),
+            dma((15,)),
+            dma,
             dma((16,)),
             dma((8,)),
             dma((8,)),
-            dma((16,)),
-            dma((16,)),
+            dma((8,)),
+            dma,
             dma((3, STEPS)),
             dma((3, STEPS)),
             dma((48,)),
@@ -378,26 +507,21 @@
         compiler_params=pltpu.CompilerParams(
             collective_id=0, has_side_effects=True, vmem_limit_bytes=32 << 20
         ),
-    )(
-        *weights,
-        mix_share.reshape(1, 448),
-        norm_train.reshape(1, 56),
-        norm_step.reshape(1, 56),
-    )
-    query, key, value = pl.pallas_call(
+    )(*inputs)
+    query, key, value, *outs = pl.pallas_call(
         write_kernel,
         out_shape=(
-            jax.ShapeDtypeStruct((7168, 896), jnp.bfloat16),
-            jax.ShapeDtypeStruct((7168, 128), jnp.bfloat16),
-            jax.ShapeDtypeStruct((7168, 128), jnp.bfloat16),
+            jax.ShapeDtypeStruct((7168, 896), bf16),
+            jax.ShapeDtypeStruct((7168, 128), bf16),
+            jax.ShapeDtypeStruct((7168, 128), bf16),
+            *small,
         ),
-        in_specs=[pl.BlockSpec(memory_space=VMEM)],
-        out_specs=(pl.BlockSpec(memory_space=HBM),) * 3,
-        scratch_shapes=[dma((24,))],
+        in_specs=[pl.BlockSpec(memory_space=VMEM)] * 5,
+        out_specs=(pl.BlockSpec(memory_space=HBM),) * 7,
+        scratch_shapes=[dma((28,))],
         compiler_params=pltpu.CompilerParams(vmem_limit_bytes=20 << 20),
-    )(gathered)
-    flat = scales.reshape(1152)
-    return (query, key, value, flat[:896], flat[896:1024], flat[1024:], gain.reshape(7168))
+    )(gathered, *rest)
+    return (query, key, value, *(x.reshape(-1) for x in outs))
 
 
 def solution(mesh):

time: 82.7 us -> 75.2 us (0.909)
  local copies, waits for them, and re-layouts: 3.71 us -> 0 us
  Pallas kernels: 78.1 us -> 74.5 us
    pallas_call x1, Pallas kernels: 72.2 us -> 68.5 us  [shards(): pl.pallas_call(gather_kernel, out_shape=(jax.ShapeDtypeStruct((7168, 1152...]
    unnamed x7 -> x0, local copies, waits for them, and re-layouts: 2.59 us -> none
    slice x2 -> x0, local copies, waits for them, and re-layouts: 1.12 us -> none  [the longest x1 0.61 us: shards(): flat[:896]]
where the time goes in v2:
time: 75.2 us; the launch traced here: 75.1 us
  Pallas kernels  74.5 us (99%)
    pallas_call x1, Pallas kernels, shards(): pl.pallas_call(gather_kernel, out_shape=(jax.ShapeDtypeStruct((7168, 1152...  68.5 us
    pallas_call x1, Pallas kernels, shards(): pl.pallas_call(write_kernel, out_shape=(jax.ShapeDtypeStruct((7168, 896),...  6.01 us

profile of v2, /device:TPU:1, one launch (start us, length us, event | category | flops | bytes accessed | tf_op | source)
XLA Modules:
  0.0 75.1 jit_solution(4564365923517700282)
XLA Ops:
  0.6 68.5 %shard_map.144 = (bf16[7168,1152]{1,0:T(8,128)(2,1)S(1)}, f32[7,128]{1,0:T(8,128)S(1)}, f32[1,128]{1,0:T(1,128)S(1)}, f32[1,128]{1,0:T(1,128)S(1)}, bf16[56,128]{1,0:T(8,128)(2,1)S(1)}) custom-call(f32[448,896]{1,0:T(8,128)} %one_query.1, f32[448,896]{1,0:T(8,128)} %other_query.1, f32[448,128]{1,0:T(8,128)} %one_key.1, f32[448,128]{1,0:T(8,128)} %other_key.1, ...), custom_call_target="tpu_custom_call" | custom-call | tf_op jit(solution)/shard_map/pallas_call | solution.py:473
  69.1 6.0 %shard_map.145 = (bf16[7168,896]{1,0:T(8,128)(2,1)}, bf16[7168,128]{1,0:T(8,128)(2,1)}, bf16[7168,128]{1,0:T(8,128)(2,1)}, f32[7,128]{1,0:T(8,128)}, f32[1,128]{...) custom-call(bf16[7168,1152]{1,0:T(8,128)(2,1)S(1)} %get-tuple-element.19.gathered, ...), custom_call_target="tpu_custom_call" | custom-call | tf_op jit(solution)/shard_map/pallas_call | solution.py:511

commit v3 on v2

v3 whole, which is shorter than its diff:
```python
import functools

import jax
import jax.numpy as jnp
from jax import lax
from jax.experimental import pallas as pl
from jax.experimental.pallas import tpu as pltpu
from jax.sharding import PartitionSpec as P

MESH = pl.DeviceIdType.MESH
HBM = pltpu.MemorySpace.HBM
VMEM = pltpu.MemorySpace.VMEM

BLOCK = 448
HALF = 224
PIECE = 112
QUERY = (0, 896)
KEYVALUE = (896, 256)
ALL = (0, 1152)
LOW = ((0, 80), (80, 144), (144, 224))
HIGH = ((224, 304), (304, 368), (368, 448))


def own(*parts):
    return [(0, 0, rows, columns) for rows, columns in parts]


def relay(dy, dz, *rows):
    return [(dy, dz, r, ALL) for r in rows]


UP = (
    own(((0, 144), KEYVALUE), ((0, 80), QUERY), ((80, 144), QUERY), (LOW[2], ALL), *((r, ALL) for r in HIGH))
    + relay(-1, 0, *LOW)
    + relay(0, 1, (224, 304), (304, 376))
    + relay(-1, 1, (0, 80), (80, 144), (144, 192), (192, 224))
)
DOWN = (
    own(((224, 368), KEYVALUE), ((224, 304), QUERY), ((304, 368), QUERY), (HIGH[2], ALL), *((r, ALL) for r in LOW))
    + relay(1, 0, *HIGH)
    + relay(0, 1, (0, 80), (80, 152))
    + relay(1, 1, (224, 304), (304, 368), (368, 416), (416, 448))
)
ACROSS = (
    own(
        ((0, 144), KEYVALUE),
        ((0, 80), QUERY),
        (HIGH[0], ALL),
        ((80, 144), QUERY),
        (HIGH[1], ALL),
        (LOW[2], ALL),
        (HIGH[2], ALL),
    )
    + relay(-1, 0, LOW[0])
    + relay(1, 0, HIGH[0])
    + relay(-1, 0, LOW[1])
    + relay(1, 0, HIGH[1])
    + relay(-1, 0, LOW[2])
    + relay(1, 0, HIGH[2])
    + relay(-1, 0, (376, 448))
    + relay(1, 0, (152, 192), (192, 224))
)
SENT = (UP, DOWN, ACROSS)
SHIFT = ((1, 0), (-1, 0), (0, 1))
STEPS = len(UP)
AHEAD = 3
SLOTS = 2 * AHEAD + 2
GATE = 5
GAIN_STEPS = (5, 8, 9, 12)
FARTHEST = ((2, 1), (1, 1), (3, 1), (2, 0), (1, 0), (3, 0), (0, 1), (0, 0))


def arriving(link, step):
    dy, dz, rows, columns = SENT[link][step]
    sy, sz = SHIFT[link]
    return ((dy - sy) % 4, (dz - sz) % 2, rows, columns)


ARRIVALS = [(l, s) for s in range(STEPS) for l in range(3)]


def needed(item):
    dy, dz, rows, _ = item
    for l, s in ARRIVALS:
        ay, az, have, _ = arriving(l, s)
        if (ay, az) == (dy % 4, dz % 2) and have[0] < rows[1] and rows[0] < have[1]:
            yield l, s


def gather_kernel(
    one_query,
    other_query,
    one_key,
    other_key,
    one_value,
    other_value,
    share_input,
    train_input,
    step_input,
    gathered,
    scale_query,
    scale_key,
    scale_value,
    gain,
    first,
    second,
    share,
    gains,
    share_row,
    share_tile,
    sums_late,
    sums_early,
    inverse,
    gain_tile,
    gain_rows,
    gain_flat,
    load_sem,
    small_sem,
    entered,
    sum_send,
    sum_recv,
    row_sem,
    gate_sem,
    gain_sem,
    link_send,
    link_recv,
    core_send,
    core_recv,
):
    me = lax.axis_index("rows")
    column = lax.axis_index("width")
    core = lax.rem(me, 2)
    y = lax.rem(me // 2, 4)
    z = me // 8

    def device(dy, dz, on):
        return lax.rem(z + dz + 2, 2) * 8 + lax.rem(y + dy + 4, 4) * 2 + on

    small = [
        pltpu.make_async_copy(share_input, share, small_sem.at[0]),
        pltpu.make_async_copy(train_input, gains.at[0], small_sem.at[1]),
        pltpu.make_async_copy(step_input, gains.at[1], small_sem.at[1]),
    ]
    pieces = BLOCK // PIECE
    small[0].start()
    for source, target, at in (
        (one_key, first, 896),
        (other_key, second, 896),
        (one_value, first, 1024),
        (other_value, second, 1024),
    ):
        pltpu.make_async_copy(source, target.at[:, pl.ds(at, 128)], load_sem.at[pieces]).start()
    for piece in range(pieces):
        rows = pl.ds(piece * PIECE, PIECE)
        for source, target in ((one_query, first), (other_query, second)):
            pltpu.make_async_copy(source.at[rows, :], target.at[rows, pl.ds(0, 896)], load_sem.at[piece]).start()
    for copy in small[1:]:
        copy.start()

    def loaded(number, rows, columns):
        place = (pl.ds(0, rows), pl.ds(0, columns))
        pltpu.make_async_copy(first.at[place], second.at[place], load_sem.at[number]).wait()

    at_gate = me == GATE
    barrier = pltpu.get_barrier_semaphore()
    for k in range(1, 16):
        peer = lax.rem(me + k, 16)

        @pl.when(peer != GATE)
        def _():
            pl.semaphore_signal(barrier, inc=1, device_id=(peer, column), device_id_type=MESH)

    @pl.when(at_gate)
    def _():
        for k in range(1, 8):
            pl.semaphore_signal(barrier, inc=1, device_id=(me, lax.rem(column + k, 8)), device_id_type=MESH)

    small[0].wait()
    share_row[...] = jnp.zeros_like(share_row)
    share_row[:, 0:BLOCK] = share[...]
    for part in range(4):
        lanes = share_row[:, part * 128 : (part + 1) * 128]
        share_tile[pl.ds(part * 128, 128), :] = jnp.transpose(jnp.broadcast_to(lanes, (128, 128)))

    def mix(start, rows, tiles, total):
        def body(i, total):
            total = list(total)
            for part in range(2):
                at = pl.ds(pl.multiple_of(start + i * 16 + part * 8, 8), 8)
                mine = share_tile[at, :]
                rest = 1.0 - mine
                for n, j in enumerate(tiles):
                    lanes = slice(j * 128, (j + 1) * 128)
                    result = mine * first[at, lanes] + rest * second[at, lanes]
                    first[at, lanes] = result
                    total[n] = total[n] + result * result
            return tuple(total)

        return lax.fori_loop(0, rows // 16, body, total, unroll=2 if len(tiles) == 2 else 1)

    def zeros(n):
        return tuple(jnp.zeros((8, 128), jnp.float32) for _ in range(n))

    others = [(dy, dz, on) for dy, dz in FARTHEST for on in (0, 1) if (dy, dz, on) != (0, 0, 0)]

    def send_sum(sums, n, dy, dz, on):
        return pltpu.make_async_remote_copy(
            src_ref=sums.at[me],
            dst_ref=sums.at[me],
            send_sem=sum_send.at[n],
            recv_sem=sum_recv.at[n],
            device_id=(device(dy, dz, lax.rem(core + on, 2)), column),
            device_id_type=MESH,
        )

    def all_sums(sums, n):
        return pltpu.make_async_remote_copy(
            src_ref=sums.at[pl.ds(0, 15)],
            dst_ref=sums.at[pl.ds(0, 15)],
            send_sem=sum_send.at[n],
            recv_sem=sum_recv.at[n],
            device_id=(device(0, 0, 1 - core), column),
            device_id_type=MESH,
        )

    def grand(sums, tiles):
        total = [sums[0, n] for n in range(len(tiles))]
        for other in range(1, 16):
            total = [t + sums[other, n] for n, t in enumerate(total)]
        for j, t in zip(tiles, total):
            scale = jnp.sqrt(t)
            if j < 7:
                scale_query[j : j + 1, :] = scale
            elif j == 7:
                scale_key[...] = scale
            else:
                scale_value[...] = scale
            inverse[j] = 1.0 / scale

    late, early = tuple(range(7)), (7, 8)

    loaded(pieces, BLOCK, 512)
    for n, t in enumerate(mix(0, BLOCK, early, zeros(2))):
        sums_early[me, n] = jnp.sum(t, axis=0, keepdims=True)

    @pl.when(jnp.logical_not(at_gate))
    def _():
        pl.semaphore_wait(barrier, 15)

    @pl.when(me == GATE - 1)
    def _():
        pl.semaphore_signal(entered, inc=1, device_id=(GATE, column), device_id_type=MESH)

    @pl.when(at_gate)
    def _():
        pl.semaphore_wait(entered, 1)

    for to in others:
        send_sum(sums_early, 0, *to).start()
    total = zeros(7)
    for piece in range(pieces):
        loaded(piece, 2 * PIECE, 896)
        total = mix(piece * PIECE, PIECE, late, total)
    for n, t in enumerate(total):
        sums_late[me, n] = jnp.sum(t, axis=0, keepdims=True)
    for to in others:
        send_sum(sums_late, 1, *to).start()

    pltpu.make_async_copy(gains, gains, small_sem.at[1]).wait()
    gain_tile[...] = jnp.zeros_like(gain_tile)
    gain_tile[0:1, 0:56] = (gains[0] + gains[1]).astype(jnp.bfloat16).astype(jnp.float32)
    place = lax.rem(56 * (lax.rem(me, 2) * 8 + column), 128)
    gain_rows[column, me] = pltpu.roll(gain_tile[...], place, 1)[0:1, :]

    def send_row():
        return pltpu.make_async_remote_copy(
            src_ref=gain_rows.at[column, me],
            dst_ref=gain_rows.at[column, me],
            send_sem=row_sem.at[0],
            recv_sem=row_sem.at[1],
            device_id=(GATE, column),
            device_id_type=MESH,
        )

    def all_rows():
        return pltpu.make_async_remote_copy(
            src_ref=gain_rows.at[column, pl.ds(0, 15)],
            dst_ref=gain_rows.at[column, pl.ds(0, 15)],
            send_sem=row_sem.at[0],
            recv_sem=row_sem.at[1],
            device_id=(GATE - 1, column),
            device_id_type=MESH,
        )

    def send_group(k):
        return pltpu.make_async_remote_copy(
            src_ref=gain_rows.at[column],
            dst_ref=gain_rows.at[column],
            send_sem=gate_sem.at[0],
            recv_sem=gate_sem.at[1],
            device_id=(GATE, lax.rem(column + k, 8)),
            device_id_type=MESH,
        )

    def all_groups():
        return pltpu.make_async_remote_copy(
            src_ref=gain_rows.at[pl.ds(0, 7)],
            dst_ref=gain_rows.at[pl.ds(0, 7)],
            send_sem=gate_sem.at[0],
            recv_sem=gate_sem.at[1],
            device_id=(GATE - 1, column),
            device_id_type=MESH,
        )

    def send_gain(to):
        return pltpu.make_async_remote_copy(
            src_ref=gain,
            dst_ref=gain,
            send_sem=gain_sem.at[0],
            recv_sem=gain_sem.at[1],
            device_id=(to, column),
            device_id_type=MESH,
        )

    def compose():
        lane = lax.broadcasted_iota(jnp.int32, (1, 128), 1)
        for group in range(8):
            rows = [jnp.zeros((1, 128), jnp.float32) for _ in range(8)]
            for j in range(16):
                values = gain_rows[j % 8, group * 2 + j // 8]
                row, at = (56 * j) // 128, (56 * j) % 128
                rows[row] = jnp.where((lane >= at) & (lane < at + 56), values, rows[row])
                if at + 56 > 128:
                    rows[row + 1] = jnp.where(lane < at + 56 - 128, values, rows[row + 1])
            for row in range(7):
                gain_flat[group * 7 + row : group * 7 + row + 1, :] = rows[row]
        gain[...] = gain_flat[...].astype(jnp.bfloat16)

    spread = [to for to in range(16) if to % 2 == GATE % 2 and to != GATE] + [GATE - 1]

    def place_of(item, on):
        dy, dz, (low, high), (left, width) = item
        start = pl.multiple_of(device(dy, dz, on) * BLOCK + low, 8)
        return (pl.ds(start, high - low), pl.ds(left, width))

    def link_copy(link, step, item):
        place = place_of(item, core)
        sy, sz = SHIFT[link]
        return pltpu.make_async_remote_copy(
            src_ref=gathered.at[place],
            dst_ref=gathered.at[place],
            send_sem=link_send.at[link, step % AHEAD],
            recv_sem=link_recv.at[link, step % SLOTS],
            device_id=(device(sy, sz, core), column),
            device_id_type=MESH,
        )

    def core_copy(place):
        return pltpu.make_async_remote_copy(
            src_ref=gathered.at[place],
            dst_ref=gathered.at[place],
            send_sem=core_send,
            recv_sem=core_recv,
            device_id=(device(0, 0, 1 - core), column),
            device_id_type=MESH,
        )

    def normalise(tiles):
        def body(i, _):
            at = pl.multiple_of(i * 16, 16)
            to = pl.multiple_of(me * BLOCK + i * 16, 16)
            for j in tiles:
                lanes = slice(j * 128, (j + 1) * 128)
                gathered[pl.ds(to, 16), lanes] = (first[pl.ds(at, 16), lanes] * inverse[j]).astype(jnp.bfloat16)
            return 0

        lax.fori_loop(0, BLOCK // 16, body, 0)

    arrived = set()

    def receive(link, step):
        if (link, step) in arrived:
            return
        arrived.add((link, step))
        item = arriving(link, step)
        link_copy(link, step, item).wait_recv()
        core_copy(place_of(item, core)).start()

    all_sums(sums_early, 0).wait_recv()
    grand(sums_early, early)
    normalise(early)

    for step in range(STEPS):
        for link in range(3):
            if step >= AHEAD:
                link_copy(link, step - AHEAD, SENT[link][step - AHEAD]).wait_send()
            item = SENT[link][step]
            if item[:2] != (0, 0):
                for arrival in needed(item):
                    receive(*arrival)
            link_copy(link, step, item).start()
        if step == 0:

            @pl.when(jnp.logical_not(at_gate))
            def _():
                send_row().start()

            all_sums(sums_late, 1).wait_recv()
            grand(sums_late, late)
            normalise(late)
        if step in (1, 2):
            core_copy(place_of((0, 0, ((step - 1) * HALF, step * HALF), ALL), core)).start()
        if step == GAIN_STEPS[0]:

            @pl.when(at_gate)
            def _():
                all_rows().wait_recv()
                pl.semaphore_wait(barrier, 7)
                for k in range(1, 8):
                    send_group(k).start()

        if step == GAIN_STEPS[1]:

            @pl.when(at_gate)
            def _():
                all_groups().wait_recv()
                compose()

        if step == GAIN_STEPS[2]:

            @pl.when(at_gate)
            def _():
                for to in spread:
                    send_gain(to).start()

        if step == GAIN_STEPS[3]:

            @pl.when(jnp.logical_and(jnp.logical_not(at_gate), core == GATE % 2))
            def _():
                send_gain(me).wait_recv()
                send_gain(device(0, 0, 1 - core)).start()

        if step >= AHEAD:
            for link in range(3):
                receive(link, step - AHEAD)

    for step in range(STEPS - AHEAD, STEPS):
        for link in range(3):
            receive(link, step)
    for step in range(STEPS - AHEAD, STEPS):
        for link in range(3):
            link_copy(link, step, SENT[link][step]).wait_send()
    all_sums(sums_early, 0).wait_send()
    all_sums(sums_late, 1).wait_send()

    @pl.when(core != GATE % 2)
    def _():
        send_gain(me).wait_recv()

    @pl.when(at_gate)
    def _():
        all_groups().wait_send()
        gains_sent = gathered.at[pl.ds(0, 448), pl.ds(0, 128)]
        pltpu.make_async_copy(gains_sent, gains_sent, gain_sem.at[0]).wait()

    @pl.when(jnp.logical_not(at_gate))
    def _():
        send_row().wait_send()

        @pl.when(core == GATE % 2)
        def _():
            send_gain(me).wait_send()

    half = core_copy((pl.ds(0, 8 * BLOCK), pl.ds(0, 1152)))
    half.wait_send()
    half.wait_recv()


def write_kernel(gathered, *rest):
    small, (query, key, value), outs, sem = rest[:4], rest[4:7], rest[7:11], rest[11]
    parts = 4
    rows = gathered.shape[0] // parts
    for part in range(parts):
        at = pl.ds(part * rows, rows)
        pltpu.make_async_copy(gathered.at[at, pl.ds(0, 896)], query.at[at, :], sem.at[0]).start()
    others = [
        pltpu.make_async_copy(gathered.at[:, pl.ds(896, 128)], key, sem.at[1]),
        pltpu.make_async_copy(gathered.at[:, pl.ds(1024, 128)], value, sem.at[2]),
    ]
    for source, target in zip(small, outs):
        others.append(pltpu.make_async_copy(source, target, sem.at[len(others) + 1]))
    for copy in others:
        copy.start()
    pltpu.make_async_copy(gathered.at[:, pl.ds(0, 896)], query, sem.at[0]).wait()
    for copy in others:
        copy.wait()


def shards(
    one_query,
    other_query,
    one_key,
    other_key,
    one_value,
    other_value,
    mix_share,
    norm_train,
    norm_step,
):
    dma = pltpu.SemaphoreType.DMA
    f32, bf16 = jnp.float32, jnp.bfloat16
    inputs = [
        pltpu.with_memory_space_constraint(x, HBM)
        for x in (
            one_query,
            other_query,
            one_key,
            other_key,
            one_value,
            other_value,
            mix_share.reshape(1, 448),
            norm_train.reshape(1, 56),
            norm_step.reshape(1, 56),
        )
    ]
    small = (
        jax.ShapeDtypeStruct((7, 128), f32),
        jax.ShapeDtypeStruct((1, 128), f32),
        jax.ShapeDtypeStruct((1, 128), f32),
        jax.ShapeDtypeStruct((56, 128), bf16),
    )
    gathered, *rest = pl.pallas_call(
        gather_kernel,
        out_shape=(jax.ShapeDtypeStruct((7168, 1152), bf16), *small),
        in_specs=[pl.BlockSpec(memory_space=HBM)] * 9,
        out_specs=(pl.BlockSpec(memory_space=VMEM),) * 5,
        scratch_shapes=[
            pltpu.VMEM((448, 1152), f32),
            pltpu.VMEM((448, 1152), f32),
            pltpu.VMEM((1, 448), f32),
            pltpu.VMEM((2, 1, 56), f32),
            pltpu.VMEM((1, 512), f32),
            pltpu.VMEM((512, 128), f32),
            pltpu.VMEM((16, 7, 1, 128), f32),
            pltpu.VMEM((16, 2, 1, 128), f32),
            pltpu.VMEM((9, 1, 128), f32),
            pltpu.VMEM((8, 128), f32),
            pltpu.VMEM((8, 16, 1, 128), f32),
            pltpu.VMEM((56, 128), f32),
            dma((BLOCK // PIECE + 1,)),
            dma((2,)),
            pltpu.SemaphoreType.REGULAR,
            dma((2,)),
            dma((2,)),
            dma((2,)),
            dma((2,)),
            dma((2,)),
            dma((3, AHEAD)),
            dma((3, SLOTS)),
            dma,
            dma,
        ],
        compiler_params=pltpu.CompilerParams(
            collective_id=0, has_side_effects=True, vmem_limit_bytes=32 << 20
        ),
    )(*inputs)
    query, key, value, *outs = pl.pallas_call(
        write_kernel,
        out_shape=(
            jax.ShapeDtypeStruct((7168, 896), bf16),
            jax.ShapeDtypeStruct((7168, 128), bf16),
            jax.ShapeDtypeStruct((7168, 128), bf16),
            *small,
        ),
        in_specs=[pl.BlockSpec(memory_space=VMEM)] * 5,
        out_specs=(pl.BlockSpec(memory_space=HBM),) * 7,
        scratch_shapes=[dma((7,))],
        compiler_params=pltpu.CompilerParams(vmem_limit_bytes=20 << 20),
    )(gathered, *rest)
    return (query, key, value, *(x.reshape(-1) for x in outs))


def solution(mesh):
    in_specs = (
        P("rows", "width"),
        P("rows", "width"),
        P("rows", "width"),
        P("rows", "width"),
        P("rows", "width"),
        P("rows", "width"),
        P("rows"),
        P(("rows", "width")),
        P(("rows", "width")),
    )
    out_specs = (
        P(None, "width"),
        P(None, "width"),
        P(None, "width"),
        P("width"),
        P("width"),
        P("width"),
        P(),
    )
    return jax.shard_map(shards, mesh=mesh, in_specs=in_specs, out_specs=out_specs, check_vma=False)
```

time: 75.2 us -> 72.6 us (0.965)
  Pallas kernels: 74.5 us -> 71.8 us
    pallas_call x1, Pallas kernels: 68.5 us -> 65.9 us  [shards(): pl.pallas_call(gather_kernel, out_shape=(jax.ShapeDtypeStruct((7168, 1152...]
where the time goes in v3:
time: 72.6 us; the launch traced here: 72.5 us
  Pallas kernels  71.8 us (99%)
    pallas_call x1, Pallas kernels, shards(): pl.pallas_call(gather_kernel, out_shape=(jax.ShapeDtypeStruct((7168, 1152...  65.9 us
    pallas_call x1, Pallas kernels, shards(): pl.pallas_call(write_kernel, out_shape=(jax.ShapeDtypeStruct((7168, 896),...  5.9 us

profile of v3, /device:TPU:1, one launch (start us, length us, event | category | flops | bytes accessed | tf_op | source)
XLA Modules:
  0.0 72.5 jit_solution(310470551216131384)
XLA Ops:
  0.6 65.9 %shard_map.144 = (bf16[7168,1152]{1,0:T(8,128)(2,1)S(1)}, f32[7,128]{1,0:T(8,128)S(1)}, f32[1,128]{1,0:T(1,128)S(1)}, f32[1,128]{1,0:T(1,128)S(1)}, bf16[56,128]{1,0:T(8,128)(2,1)S(1)}) custom-call(f32[448,896]{1,0:T(8,128)} %one_query.1, f32[448,896]{1,0:T(8,128)} %other_query.1, f32[448,128]{1,0:T(8,128)} %one_key.1, f32[448,128]{1,0:T(8,128)} %other_key.1, ...), custom_call_target="tpu_custom_call" | custom-call | tf_op jit(solution)/shard_map/pallas_call | solution.py:532
  66.6 5.9 %shard_map.145 = (bf16[7168,896]{1,0:T(8,128)(2,1)}, bf16[7168,128]{1,0:T(8,128)(2,1)}, bf16[7168,128]{1,0:T(8,128)(2,1)}, f32[7,128]{1,0:T(8,128)}, f32[1,128]{...) custom-call(bf16[7168,1152]{1,0:T(8,128)(2,1)S(1)} %get-tuple-element.19.gathered, ...), custom_call_target="tpu_custom_call" | custom-call | tf_op jit(solution)/shard_map/pallas_call | solution.py:567

commit v4 on v3

--- a/solution.py
+++ b/solution.py
@@ -17,7 +17,8 @@
 QUERY = (0, 896)
 KEYVALUE = (896, 256)
 ALL = (0, 1152)
-LOW = ((0, 80), (80, 144), (144, 224))
+EARLY = 32
+LOW = ((EARLY, 96), (96, 160), (160, 224))
 HIGH = ((224, 304), (304, 368), (368, 448))
 
 
@@ -30,40 +31,40 @@
 
 
 UP = (
-    own(((0, 144), KEYVALUE), ((0, 80), QUERY), ((80, 144), QUERY), (LOW[2], ALL), *((r, ALL) for r in HIGH))
-    + relay(-1, 0, *LOW)
+    own(((EARLY, 160), KEYVALUE), (LOW[0], QUERY), (LOW[1], QUERY), (LOW[2], ALL), *((r, ALL) for r in HIGH))
+    + relay(-1, 0, (0, 96), *LOW[1:])
     + relay(0, 1, (224, 304), (304, 376))
-    + relay(-1, 1, (0, 80), (80, 144), (144, 192), (192, 224))
+    + relay(-1, 1, (0, 96), (96, 160), (160, 208), (208, 224))
 )
 DOWN = (
-    own(((224, 368), KEYVALUE), ((224, 304), QUERY), ((304, 368), QUERY), (HIGH[2], ALL), *((r, ALL) for r in LOW))
+    own(((224, 368), KEYVALUE), (HIGH[0], QUERY), (HIGH[1], QUERY), (HIGH[2], ALL), *((r, ALL) for r in LOW))
     + relay(1, 0, *HIGH)
     + relay(0, 1, (0, 80), (80, 152))
-    + relay(1, 1, (224, 304), (304, 368), (368, 416), (416, 448))
+    + relay(1, 1, (224, 304), (304, 368), (368, 432), (432, 448))
 )
 ACROSS = (
     own(
-        ((0, 144), KEYVALUE),
-        ((0, 80), QUERY),
+        ((EARLY, 160), KEYVALUE),
+        (LOW[0], QUERY),
         (HIGH[0], ALL),
-        ((80, 144), QUERY),
+        (LOW[1], QUERY),
         (HIGH[1], ALL),
         (LOW[2], ALL),
         (HIGH[2], ALL),
     )
-    + relay(-1, 0, LOW[0])
+    + relay(-1, 0, (0, 96))
     + relay(1, 0, HIGH[0])
     + relay(-1, 0, LOW[1])
     + relay(1, 0, HIGH[1])
     + relay(-1, 0, LOW[2])
     + relay(1, 0, HIGH[2])
     + relay(-1, 0, (376, 448))
-    + relay(1, 0, (152, 192), (192, 224))
+    + relay(1, 0, (152, 208), (208, 224))
 )
 SENT = (UP, DOWN, ACROSS)
 SHIFT = ((1, 0), (-1, 0), (0, 1))
 STEPS = len(UP)
-AHEAD = 3
+AHEAD = 2
 SLOTS = 2 * AHEAD + 2
 GATE = 5
 GAIN_STEPS = (5, 8, 9, 12)
@@ -114,6 +115,7 @@
     gain_tile,
     gain_rows,
     gain_flat,
+    early_rows,
     load_sem,
     small_sem,
     entered,
@@ -126,6 +128,7 @@
     link_recv,
     core_send,
     core_recv,
+    early_sem,
 ):
     me = lax.axis_index("rows")
     column = lax.axis_index("width")
@@ -135,6 +138,21 @@
 
     def device(dy, dz, on):
         return lax.rem(z + dz + 2, 2) * 8 + lax.rem(y + dy + 4, 4) * 2 + on
+
+    at_gate = me == GATE
+    barrier = pltpu.get_barrier_semaphore()
+    others = [(dy, dz, on) for dy, dz in FARTHEST for on in (0, 1) if (dy, dz, on) != (0, 0, 0)]
+    for dy, dz, on in others:
+        peer = device(dy, dz, lax.rem(core + on, 2))
+
+        @pl.when(peer != GATE)
+        def _():
+            pl.semaphore_signal(barrier, inc=1, device_id=(peer, column), device_id_type=MESH)
+
+    @pl.when(at_gate)
+    def _():
+        for k in range(1, 8):
+            pl.semaphore_signal(barrier, inc=1, device_id=(me, lax.rem(column + k, 8)), device_id_type=MESH)
 
     small = [
         pltpu.make_async_copy(share_input, share, small_sem.at[0]),
@@ -161,20 +179,6 @@
         place = (pl.ds(0, rows), pl.ds(0, columns))
         pltpu.make_async_copy(first.at[place], second.at[place], load_sem.at[number]).wait()
 
-    at_gate = me == GATE
-    barrier = pltpu.get_barrier_semaphore()
-    for k in range(1, 16):
-        peer = lax.rem(me + k, 16)
-
-        @pl.when(peer != GATE)
-        def _():
-            pl.semaphore_signal(barrier, inc=1, device_id=(peer, column), device_id_type=MESH)
-
-    @pl.when(at_gate)
-    def _():
-        for k in range(1, 8):
-            pl.semaphore_signal(barrier, inc=1, device_id=(me, lax.rem(column + k, 8)), device_id_type=MESH)
-
     small[0].wait()
     share_row[...] = jnp.zeros_like(share_row)
     share_row[:, 0:BLOCK] = share[...]
@@ -201,8 +205,6 @@
     def zeros(n):
         return tuple(jnp.zeros((8, 128), jnp.float32) for _ in range(n))
 
-    others = [(dy, dz, on) for dy, dz in FARTHEST for on in (0, 1) if (dy, dz, on) != (0, 0, 0)]
-
     def send_sum(sums, n, dy, dz, on):
         return pltpu.make_async_remote_copy(
             src_ref=sums.at[me],
@@ -266,6 +268,30 @@
     for to in others:
         send_sum(sums_late, 1, *to).start()
 
+    def early_copy(link):
+        sy, sz = SHIFT[link]
+        return pltpu.make_async_remote_copy(
+            src_ref=first.at[pl.ds(0, EARLY), :],
+            dst_ref=early_rows.at[link],
+            send_sem=early_sem.at[0],
+            recv_sem=early_sem.at[1],
+            device_id=(device(sy, sz, core), column),
+            device_id_type=MESH,
+        )
+
+    def all_early():
+        return pltpu.make_async_remote_copy(
+            src_ref=early_rows,
+            dst_ref=early_rows,
+            send_sem=early_sem.at[0],
+            recv_sem=early_sem.at[1],
+            device_id=(device(0, 0, 1 - core), column),
+            device_id_type=MESH,
+        )
+
+    for link in range(3):
+        early_copy(link).start()
+
     pltpu.make_async_copy(gains, gains, small_sem.at[1]).wait()
     gain_tile[...] = jnp.zeros_like(gain_tile)
     gain_tile[0:1, 0:56] = (gains[0] + gains[1]).astype(jnp.bfloat16).astype(jnp.float32)
@@ -376,6 +402,15 @@
 
         lax.fori_loop(0, BLOCK // 16, body, 0)
 
+    def normalise_early():
+        for link, (sy, sz) in enumerate(SHIFT):
+            for i in range(EARLY // 16):
+                to = pl.multiple_of(device(-sy, -sz, core) * BLOCK + i * 16, 16)
+                for j in range(9):
+                    lanes = slice(j * 128, (j + 1) * 128)
+                    values = early_rows[link, i * 16 : (i + 1) * 16, lanes] * inverse[j]
+                    gathered[pl.ds(to, 16), lanes] = values.astype(jnp.bfloat16)
+
     arrived = set()
 
     def receive(link, step):
@@ -408,6 +443,12 @@
             all_sums(sums_late, 1).wait_recv()
             grand(sums_late, late)
             normalise(late)
+        if step == 1:
+            all_early().wait_recv()
+            normalise_early()
+        if step == 3:
+            for sy, sz in SHIFT:
+                core_copy(place_of((-sy, -sz, (0, EARLY), ALL), core)).start()
         if step in (1, 2):
             core_copy(place_of((0, 0, ((step - 1) * HALF, step * HALF), ALL), core)).start()
         if step == GAIN_STEPS[0]:
@@ -450,6 +491,7 @@
     for step in range(STEPS - AHEAD, STEPS):
         for link in range(3):
             link_copy(link, step, SENT[link][step]).wait_send()
+    all_early().wait_send()
     all_sums(sums_early, 0).wait_send()
     all_sums(sums_late, 1).wait_send()
 
@@ -547,6 +589,7 @@
             pltpu.VMEM((8, 128), f32),
             pltpu.VMEM((8, 16, 1, 128), f32),
             pltpu.VMEM((56, 128), f32),
+            pltpu.VMEM((3, EARLY, 1152), f32),
             dma((BLOCK // PIECE + 1,)),
             dma((2,)),
             pltpu.SemaphoreType.REGULAR,
@@ -559,6 +602,7 @@
             dma((3, SLOTS)),
             dma,
             dma,
+            dma((2,)),
         ],
         compiler_params=pltpu.CompilerParams(
             collective_id=0, has_side_effects=True, vmem_limit_bytes=32 << 20

time: 72.6 us -> 71.1 us (0.979)
  Pallas kernels: 71.8 us -> 70.3 us
    pallas_call x1, Pallas kernels: 65.9 us -> 64.4 us  [shards(): pl.pallas_call(gather_kernel, out_shape=(jax.ShapeDtypeStruct((7168, 1152...]
where the time goes in v4:
time: 71.1 us; the launch traced here: 71 us
  Pallas kernels  70.3 us (99%)
    pallas_call x1, Pallas kernels, shards(): pl.pallas_call(gather_kernel, out_shape=(jax.ShapeDtypeStruct((7168, 1152...  64.4 us
    pallas_call x1, Pallas kernels, shards(): pl.pallas_call(write_kernel, out_shape=(jax.ShapeDtypeStruct((7168, 896),...  5.9 us

profile of v4, /device:TPU:1, one launch (start us, length us, event | category | flops | bytes accessed | tf_op | source)
XLA Modules:
  0.0 71.0 jit_solution(12675851321837377837)
XLA Ops:
  0.6 64.4 %shard_map.144 = (bf16[7168,1152]{1,0:T(8,128)(2,1)S(1)}, f32[7,128]{1,0:T(8,128)S(1)}, f32[1,128]{1,0:T(1,128)S(1)}, f32[1,128]{1,0:T(1,128)S(1)}, bf16[56,128]{1,0:T(8,128)(2,1)S(1)}) custom-call(f32[448,896]{1,0:T(8,128)} %one_query.1, f32[448,896]{1,0:T(8,128)} %other_query.1, f32[448,128]{1,0:T(8,128)} %one_key.1, f32[448,128]{1,0:T(8,128)} %other_key.1, ...), custom_call_target="tpu_custom_call" | custom-call | tf_op jit(solution)/shard_map/pallas_call | solution.py:574
  65.1 5.9 %shard_map.145 = (bf16[7168,896]{1,0:T(8,128)(2,1)}, bf16[7168,128]{1,0:T(8,128)(2,1)}, bf16[7168,128]{1,0:T(8,128)(2,1)}, f32[7,128]{1,0:T(8,128)}, f32[1,128]{...) custom-call(bf16[7168,1152]{1,0:T(8,128)(2,1)S(1)} %get-tuple-element.19.gathered, ...), custom_call_target="tpu_custom_call" | custom-call | tf_op jit(solution)/shard_map/pallas_call | solution.py:611

commit v5 on v4

--- a/solution.py
+++ b/solution.py
@@ -18,6 +18,7 @@
 KEYVALUE = (896, 256)
 ALL = (0, 1152)
 EARLY = 32
+LAST = 8
 LOW = ((EARLY, 96), (96, 160), (160, 224))
 HIGH = ((224, 304), (304, 368), (368, 448))
 
@@ -34,13 +35,13 @@
     own(((EARLY, 160), KEYVALUE), (LOW[0], QUERY), (LOW[1], QUERY), (LOW[2], ALL), *((r, ALL) for r in HIGH))
     + relay(-1, 0, (0, 96), *LOW[1:])
     + relay(0, 1, (224, 304), (304, 376))
-    + relay(-1, 1, (0, 96), (96, 160), (160, 208), (208, 224))
+    + relay(-1, 1, (0, 96), (96, 160), (160, 200), (200, 216), (216, 224))
 )
 DOWN = (
     own(((224, 368), KEYVALUE), (HIGH[0], QUERY), (HIGH[1], QUERY), (HIGH[2], ALL), *((r, ALL) for r in LOW))
     + relay(1, 0, *HIGH)
     + relay(0, 1, (0, 80), (80, 152))
-    + relay(1, 1, (224, 304), (304, 368), (368, 432), (432, 448))
+    + relay(1, 1, (224, 304), (304, 368), (368, 424), (424, 440), (440, 448))
 )
 ACROSS = (
     own(
@@ -59,7 +60,7 @@
     + relay(-1, 0, LOW[2])
     + relay(1, 0, HIGH[2])
     + relay(-1, 0, (376, 448))
-    + relay(1, 0, (152, 208), (208, 224))
+    + relay(1, 0, (152, 200), (200, 216), (216, 224))
 )
 SENT = (UP, DOWN, ACROSS)
 SHIFT = ((1, 0), (-1, 0), (0, 1))
@@ -129,6 +130,7 @@
     core_send,
     core_recv,
     early_sem,
+    last_sem,
 ):
     me = lax.axis_index("rows")
     column = lax.axis_index("width")
@@ -381,6 +383,18 @@
             device_id_type=MESH,
         )
 
+    def last_copy(link):
+        place = place_of(SENT[link][STEPS - 1], core)
+        sy, sz = SHIFT[link]
+        return pltpu.make_async_remote_copy(
+            src_ref=gathered.at[place],
+            dst_ref=gathered.at[place],
+            send_sem=last_sem.at[0],
+            recv_sem=last_sem.at[1],
+            device_id=(device(sy, sz, 1 - core), column),
+            device_id_type=MESH,
+        )
+
     def core_copy(place):
         return pltpu.make_async_remote_copy(
             src_ref=gathered.at[place],
@@ -419,7 +433,8 @@
         arrived.add((link, step))
         item = arriving(link, step)
         link_copy(link, step, item).wait_recv()
-        core_copy(place_of(item, core)).start()
+        if step < STEPS - 1:
+            core_copy(place_of(item, core)).start()
 
     all_sums(sums_early, 0).wait_recv()
     grand(sums_early, early)
@@ -434,6 +449,8 @@
                 for arrival in needed(item):
                     receive(*arrival)
             link_copy(link, step, item).start()
+            if step == STEPS - 1:
+                last_copy(link).start()
         if step == 0:
 
             @pl.when(jnp.logical_not(at_gate))
@@ -513,9 +530,12 @@
         def _():
             send_gain(me).wait_send()
 
-    half = core_copy((pl.ds(0, 8 * BLOCK), pl.ds(0, 1152)))
+    half = core_copy((pl.ds(0, 8 * BLOCK - 3 * LAST), pl.ds(0, 1152)))
     half.wait_send()
     half.wait_recv()
+    rows = gathered.at[pl.ds(0, 3 * LAST), :]
+    for n in range(2):
+        pltpu.make_async_copy(rows, rows, last_sem.at[n]).wait()
 
 
 def write_kernel(gathered, *rest):
@@ -603,6 +623,7 @@
             dma,
             dma,
             dma((2,)),
+            dma((2,)),
         ],
         compiler_params=pltpu.CompilerParams(
             collective_id=0, has_side_effects=True, vmem_limit_bytes=32 << 20

time: 71.1 us -> 70.6 us (level)
  no operation moved by 1% of the time
where the time goes in v5:
time: 70.6 us; the launch traced here: 70.5 us
  Pallas kernels  69.9 us (99%)
    pallas_call x1, Pallas kernels, shards(): pl.pallas_call(gather_kernel, out_shape=(jax.ShapeDtypeStruct((7168, 1152...  64 us
    pallas_call x1, Pallas kernels, shards(): pl.pallas_call(write_kernel, out_shape=(jax.ShapeDtypeStruct((7168, 896),...  5.9 us

profile of v5, /device:TPU:1, one launch (start us, length us, event | category | flops | bytes accessed | tf_op | source)
XLA Modules:
  0.0 70.5 jit_solution(16560556012154427513)
XLA Ops:
  0.6 64.0 %shard_map.144 = (bf16[7168,1152]{1,0:T(8,128)(2,1)S(1)}, f32[7,128]{1,0:T(8,128)S(1)}, f32[1,128]{1,0:T(1,128)S(1)}, f32[1,128]{1,0:T(1,128)S(1)}, bf16[56,128]{1,0:T(8,128)(2,1)S(1)}) custom-call(f32[448,896]{1,0:T(8,128)} %one_query.1, f32[448,896]{1,0:T(8,128)} %other_query.1, f32[448,128]{1,0:T(8,128)} %one_key.1, f32[448,128]{1,0:T(8,128)} %other_key.1, ...), custom_call_target="tpu_custom_call" | custom-call | tf_op jit(solution)/shard_map/pallas_call | solution.py:594
  64.6 5.9 %shard_map.145 = (bf16[7168,896]{1,0:T(8,128)(2,1)}, bf16[7168,128]{1,0:T(8,128)(2,1)}, bf16[7168,128]{1,0:T(8,128)(2,1)}, f32[7,128]{1,0:T(8,128)}, f32[1,128]{...) custom-call(bf16[7168,1152]{1,0:T(8,128)(2,1)S(1)} %get-tuple-element.19.gathered, ...), custom_call_target="tpu_custom_call" | custom-call | tf_op jit(solution)/shard_map/pallas_call | solution.py:632

commit v6 on v5

--- a/solution.py
+++ b/solution.py
@@ -67,7 +67,7 @@
 STEPS = len(UP)
 AHEAD = 2
 SLOTS = 2 * AHEAD + 2
-GATE = 5
+GATE = 1
 GAIN_STEPS = (5, 8, 9, 12)
 FARTHEST = ((2, 1), (1, 1), (3, 1), (2, 0), (1, 0), (3, 0), (0, 1), (0, 0))
 
@@ -144,17 +144,15 @@
     at_gate = me == GATE
     barrier = pltpu.get_barrier_semaphore()
     others = [(dy, dz, on) for dy, dz in FARTHEST for on in (0, 1) if (dy, dz, on) != (0, 0, 0)]
-    for dy, dz, on in others:
-        peer = device(dy, dz, lax.rem(core + on, 2))
-
-        @pl.when(peer != GATE)
-        def _():
-            pl.semaphore_signal(barrier, inc=1, device_id=(peer, column), device_id_type=MESH)
-
-    @pl.when(at_gate)
-    def _():
-        for k in range(1, 8):
-            pl.semaphore_signal(barrier, inc=1, device_id=(me, lax.rem(column + k, 8)), device_id_type=MESH)
+    def signal(peers):
+        for dy, dz, on in peers:
+            peer = device(dy, dz, lax.rem(core + on, 2))
+
+            @pl.when(peer != GATE)
+            def _():
+                pl.semaphore_signal(barrier, inc=1, device_id=(peer, column), device_id_type=MESH)
+
+    signal(others[:6])
 
     small = [
         pltpu.make_async_copy(share_input, share, small_sem.at[0]),
@@ -176,6 +174,13 @@
             pltpu.make_async_copy(source.at[rows, :], target.at[rows, pl.ds(0, 896)], load_sem.at[piece]).start()
     for copy in small[1:]:
         copy.start()
+
+    signal(others[6:])
+
+    @pl.when(at_gate)
+    def _():
+        for k in range(1, 8):
+            pl.semaphore_signal(barrier, inc=1, device_id=(me, lax.rem(column + k, 8)), device_id_type=MESH)
 
     def loaded(number, rows, columns):
         place = (pl.ds(0, rows), pl.ds(0, columns))

time: 70.6 us -> 70.3 us (level)
  no operation moved by 1% of the time
where the time goes in v6:
time: 70.3 us; the launch traced here: 70.2 us
  Pallas kernels  69.6 us (99%)
    pallas_call x1, Pallas kernels, shards(): pl.pallas_call(gather_kernel, out_shape=(jax.ShapeDtypeStruct((7168, 1152...  63.7 us
    pallas_call x1, Pallas kernels, shards(): pl.pallas_call(write_kernel, out_shape=(jax.ShapeDtypeStruct((7168, 896),...  5.9 us

profile of v6, /device:TPU:1, one launch (start us, length us, event | category | flops | bytes accessed | tf_op | source)
XLA Modules:
  0.0 70.2 jit_solution(9123965511386017837)
XLA Ops:
  0.6 63.7 %shard_map.144 = (bf16[7168,1152]{1,0:T(8,128)(2,1)S(1)}, f32[7,128]{1,0:T(8,128)S(1)}, f32[1,128]{1,0:T(1,128)S(1)}, f32[1,128]{1,0:T(1,128)S(1)}, bf16[56,128]{1,0:T(8,128)(2,1)S(1)}) custom-call(f32[448,896]{1,0:T(8,128)} %one_query.1, f32[448,896]{1,0:T(8,128)} %other_query.1, f32[448,128]{1,0:T(8,128)} %one_key.1, f32[448,128]{1,0:T(8,128)} %other_key.1, ...), custom_call_target="tpu_custom_call" | custom-call | tf_op jit(solution)/shard_map/pallas_call | solution.py:599
  64.3 5.9 %shard_map.145 = (bf16[7168,896]{1,0:T(8,128)(2,1)}, bf16[7168,128]{1,0:T(8,128)(2,1)}, bf16[7168,128]{1,0:T(8,128)(2,1)}, f32[7,128]{1,0:T(8,128)}, f32[1,128]{...) custom-call(bf16[7168,1152]{1,0:T(8,128)(2,1)S(1)} %get-tuple-element.19.gathered, ...), custom_call_target="tpu_custom_call" | custom-call | tf_op jit(solution)/shard_map/pallas_call | solution.py:637

commit v7 on v6

--- a/solution.py
+++ b/solution.py
@@ -32,25 +32,25 @@
 
 
 UP = (
-    own(((EARLY, 160), KEYVALUE), (LOW[0], QUERY), (LOW[1], QUERY), (LOW[2], ALL), *((r, ALL) for r in HIGH))
+    own(((EARLY, 224), KEYVALUE), (LOW[0], QUERY), (LOW[1], QUERY), (LOW[2], QUERY), *((r, ALL) for r in HIGH))
     + relay(-1, 0, (0, 96), *LOW[1:])
     + relay(0, 1, (224, 304), (304, 376))
     + relay(-1, 1, (0, 96), (96, 160), (160, 200), (200, 216), (216, 224))
 )
 DOWN = (
-    own(((224, 368), KEYVALUE), (HIGH[0], QUERY), (HIGH[1], QUERY), (HIGH[2], ALL), *((r, ALL) for r in LOW))
+    own(((224, 448), KEYVALUE), (HIGH[0], QUERY), (HIGH[1], QUERY), (HIGH[2], QUERY), *((r, ALL) for r in LOW))
     + relay(1, 0, *HIGH)
     + relay(0, 1, (0, 80), (80, 152))
     + relay(1, 1, (224, 304), (304, 368), (368, 424), (424, 440), (440, 448))
 )
 ACROSS = (
     own(
-        ((EARLY, 160), KEYVALUE),
+        ((EARLY, 224), KEYVALUE),
         (LOW[0], QUERY),
         (HIGH[0], ALL),
         (LOW[1], QUERY),
         (HIGH[1], ALL),
-        (LOW[2], ALL),
+        (LOW[2], QUERY),
         (HIGH[2], ALL),
     )
     + relay(-1, 0, (0, 96))

time: 70.3 us -> 70.3 us (level)
  no operation moved by 1% of the time
where the time goes in v7:
time: 70.3 us; the launch traced here: 70.2 us
  Pallas kernels  69.6 us (99%)
    pallas_call x1, Pallas kernels, shards(): pl.pallas_call(gather_kernel, out_shape=(jax.ShapeDtypeStruct((7168, 1152...  63.7 us
    pallas_call x1, Pallas kernels, shards(): pl.pallas_call(write_kernel, out_shape=(jax.ShapeDtypeStruct((7168, 896),...  5.9 us

profile of v7, /device:TPU:1, one launch (start us, length us, event | category | flops | bytes accessed | tf_op | source)
XLA Modules:
  0.0 70.2 jit_solution(9029246496310717965)
XLA Ops:
  0.6 63.7 %shard_map.144 = (bf16[7168,1152]{1,0:T(8,128)(2,1)S(1)}, f32[7,128]{1,0:T(8,128)S(1)}, f32[1,128]{1,0:T(1,128)S(1)}, f32[1,128]{1,0:T(1,128)S(1)}, bf16[56,128]{1,0:T(8,128)(2,1)S(1)}) custom-call(f32[448,896]{1,0:T(8,128)} %one_query.1, f32[448,896]{1,0:T(8,128)} %other_query.1, f32[448,128]{1,0:T(8,128)} %one_key.1, f32[448,128]{1,0:T(8,128)} %other_key.1, ...), custom_call_target="tpu_custom_call" | custom-call | tf_op jit(solution)/shard_map/pallas_call | solution.py:599
  64.3 5.9 %shard_map.145 = (bf16[7168,896]{1,0:T(8,128)(2,1)}, bf16[7168,128]{1,0:T(8,128)(2,1)}, bf16[7168,128]{1,0:T(8,128)(2,1)}, f32[7,128]{1,0:T(8,128)}, f32[1,128]{...) custom-call(bf16[7168,1152]{1,0:T(8,128)(2,1)S(1)} %get-tuple-element.19.gathered, ...), custom_call_target="tpu_custom_call" | custom-call | tf_op jit(solution)/shard_map/pallas_call | solution.py:637

commit v8 on v6

--- a/solution.py
+++ b/solution.py
@@ -69,7 +69,7 @@
 SLOTS = 2 * AHEAD + 2
 GATE = 1
 GAIN_STEPS = (5, 8, 9, 12)
-FARTHEST = ((2, 1), (1, 1), (3, 1), (2, 0), (1, 0), (3, 0), (0, 1), (0, 0))
+FARTHEST = ((2, 1), (2, 0), (1, 1), (3, 1), (1, 0), (3, 0), (0, 1), (0, 0))
 
 
 def arriving(link, step):

time: 70.3 us -> 70.3 us (level)
  no operation moved by 1% of the time
where the time goes in v8:
time: 70.3 us; the launch traced here: 70.2 us
  Pallas kernels  69.6 us (99%)
    pallas_call x1, Pallas kernels, shards(): pl.pallas_call(gather_kernel, out_shape=(jax.ShapeDtypeStruct((7168, 1152...  63.7 us
    pallas_call x1, Pallas kernels, shards(): pl.pallas_call(write_kernel, out_shape=(jax.ShapeDtypeStruct((7168, 896),...  5.9 us

profile of v8, /device:TPU:1, one launch (start us, length us, event | category | flops | bytes accessed | tf_op | source)
XLA Modules:
  0.0 70.2 jit_solution(12543791676636376118)
XLA Ops:
  0.6 63.7 %shard_map.144 = (bf16[7168,1152]{1,0:T(8,128)(2,1)S(1)}, f32[7,128]{1,0:T(8,128)S(1)}, f32[1,128]{1,0:T(1,128)S(1)}, f32[1,128]{1,0:T(1,128)S(1)}, bf16[56,128]{1,0:T(8,128)(2,1)S(1)}) custom-call(f32[448,896]{1,0:T(8,128)} %one_query.1, f32[448,896]{1,0:T(8,128)} %other_query.1, f32[448,128]{1,0:T(8,128)} %one_key.1, f32[448,128]{1,0:T(8,128)} %other_key.1, ...), custom_call_target="tpu_custom_call" | custom-call | tf_op jit(solution)/shard_map/pallas_call | solution.py:599
  64.3 5.9 %shard_map.145 = (bf16[7168,896]{1,0:T(8,128)(2,1)}, bf16[7168,128]{1,0:T(8,128)(2,1)}, bf16[7168,128]{1,0:T(8,128)(2,1)}, f32[7,128]{1,0:T(8,128)}, f32[1,128]{...) custom-call(bf16[7168,1152]{1,0:T(8,128)(2,1)S(1)} %get-tuple-element.19.gathered, ...), custom_call_target="tpu_custom_call" | custom-call | tf_op jit(solution)/shard_map/pallas_call | solution.py:637
